TPU v7x, 256 devices: a whole 4x4x8 slice. The times are simulated.
256 devices in a mesh: dp: 16 (over z, x_lo), rep: 4 (over y), ind: 4 (over x_hi, core).
Axes of the slice: x: 4 (x_hi: 2, x_lo: 2; x = x_hi * 2 + x_lo), y: 4, z: 8, core: 2. Of those that a mesh axis runs over, the one named last changes fastest.
Arguments:
- points: bfloat16 [49152, 64], P(('dp', 'rep')), may hold values from -6 to 6
- targets: float32 [49152], P(('dp', 'rep')), may hold values from -6 to 6
- inducing: float32 [4096, 64], P('ind'), may hold values from -6 to 6
- whitening: bfloat16 [4096, 4096], P('ind'), may hold values from -0.01953125 to 0.01953125
- mean_v: float32 [4096], P('ind'), may hold values from -12 to 12
- covariance: float32 [4096, 4096], P('ind', ('dp', 'rep')), may hold values from -24 to 24
- precision: float32 [4096, 4096], P('ind', ('dp', 'rep')), may hold values from -3 to 3
- natural_one: float32 [4096], P('ind'), may hold values from -6 to 6
- lengthscales: float32 [64], replicated, may hold values from 1.6 to 24
- hypers: float32 [2], replicated, may hold values from 0.5 to 2
Outputs:
- precision_new: float32 [4096, 4096], P('ind', ('dp', 'rep'))
- natural_new: float32 [4096], P('ind')
- expected_fit: float32 [], replicated
All inputs are finite; a program needn't handle non-finite values.
Results may differ from a plain program's by a relative error of at most 0.0076.
Values may be sent and summed in bfloat16 or wider, within the bound.
A program may use at most 128 MiB of HBM per device.

v0:
```python
import functools

import jax
import jax.numpy as jnp
from jax import lax
from jax.sharding import Mesh
from jax.sharding import PartitionSpec as P

IND = ("ind_0", "ind_1")
DP_REP = ("dp_0", "dp_1", "rep")
DP_REP_IND = ("dp_0", "dp_1", "rep", "ind_0", "ind_1")


def joined_along(blocks, dim):
    shape = list(blocks.shape[1:])
    shape[dim] *= blocks.shape[0]
    return jnp.moveaxis(blocks, 0, dim).reshape(shape)


def sent_to_all(array, axis):
    copies = jnp.broadcast_to(array, (lax.axis_size(axis), *array.shape))
    return lax.all_to_all(copies, axis, split_axis=0, concat_axis=0, tiled=True)


def collect(array, axis, dim):
    return joined_along(sent_to_all(array, axis), dim)


def of_everyone(array, axis):
    return sent_to_all(array, axis).sum(axis=0)


def together(arrays, axis):
    ends = [0]
    for a in arrays:
        ends.append(ends[-1] + a.size)
    total = of_everyone(jnp.concatenate([a.ravel() for a in arrays]), axis)
    return tuple((total[b:e].reshape(a.shape) for a, b, e in zip(arrays, ends, ends[1:])))


def sum_in_order(blocks, axes, sequence):
    inside = blocks.shape[1:]
    blocks = blocks.reshape(*(lax.axis_size(a) for a in axes), *inside)
    blocks = jnp.moveaxis(blocks, sequence, range(len(axes))).reshape(-1, *inside)
    for k in sequence:
        blocks = lax.psum_scatter(blocks, axes[k], scatter_dimension=0, tiled=True)
    return blocks[0]


def cut_along(array, dim, length):
    before, after = (array.shape[:dim], array.shape[dim + 1 :])
    return jnp.moveaxis(array.reshape(*before, length, -1, *after), dim, 0)


def summed_rows(array, axes, sequence, dim):
    length = lax.axis_size(axes)
    return sum_in_order(cut_along(array, dim, length), axes, sequence)


def one_axis_at_a_time(array, axes):
    return functools.reduce(lax.psum, axes, array)


def cross_cov(inducing, points, lengthscales, signal):
    scaled_z = inducing / lengthscales
    scaled_x = points.astype(jnp.float32) / lengthscales
    norm_z = jnp.sum(scaled_z * scaled_z, axis=1)
    norm_x = jnp.sum(scaled_x * scaled_x, axis=1)
    inner = jnp.dot(scaled_z, scaled_x.T, precision=lax.Precision.HIGHEST)
    return (signal * jnp.exp(-0.5 * (norm_z[:, None] + norm_x[None, :] - 2.0 * inner))).astype(
        jnp.bfloat16
    )


def shards(
    points,
    targets,
    inducing,
    whitening,
    mean_v,
    covariance,
    precision,
    natural_one,
    lengthscales,
    hypers,
):
    signal = hypers[0]
    noise_var = hypers[1]
    all_inducing = collect(inducing, IND, 0)
    cross = cross_cov(all_inducing, points, lengthscales, signal)
    white = jnp.dot(whitening, cross, preferred_element_type=jnp.float32).astype(jnp.bfloat16)
    white_wide = white.astype(jnp.float32)
    mean_part = jnp.dot(mean_v, white_wide, precision=lax.Precision.HIGHEST)
    square_part = jnp.sum(white_wide * white_wide, axis=0)
    gram_part = lax.dot_general(
        white,
        lax.all_gather(white, IND, axis=0, tiled=True),
        (((1,), (1,)), ((), ())),
        preferred_element_type=jnp.float32,
    )
    pred_mean, sq_norm = together((mean_part, square_part), IND)
    resid = targets - pred_mean
    local_fit = jnp.sum(resid * resid + signal - sq_norm)
    local_proj = jnp.dot(white_wide, targets, precision=lax.Precision.HIGHEST)
    proj, fit_sum = together((local_proj, local_fit), DP_REP)
    own_rows = gram_part.shape[0]
    gram = summed_rows(gram_part.astype(jnp.bfloat16), DP_REP, (2, 0, 1), 1).astype(jnp.float32)
    own_cols = gram.shape[1]
    trace = one_axis_at_a_time(jnp.sum(covariance * gram), DP_REP_IND)
    total = points.shape[0] * lax.axis_size(DP_REP)
    expected_fit = -0.5 * jnp.log(2.0 * jnp.pi * noise_var) - (fit_sum + trace) / (
        2.0 * noise_var * total
    )
    row_ids = lax.axis_index(IND) * own_rows + jnp.arange(own_rows, dtype=jnp.int32)
    col_ids = lax.axis_index(DP_REP) * own_cols + jnp.arange(own_cols, dtype=jnp.int32)
    identity = (row_ids[:, None] == col_ids[None, :]).astype(jnp.float32)
    precision_new = 0.5 * precision + 0.5 * (identity + gram / noise_var)
    natural_new = 0.5 * natural_one + 0.5 * proj / noise_var
    return (precision_new, natural_new, expected_fit)


def solution(mesh):
    finer = Mesh(
        mesh.devices.reshape(8, 2, mesh.shape["rep"], 2, 2),
        ("dp_0", "dp_1", "rep", "ind_0", "ind_1"),
    )
    return jax.shard_map(
        shards,
        mesh=finer,
        in_specs=(
            P(DP_REP, None),
            P(DP_REP),
            P(IND, None),
            P(IND, None),
            P(IND),
            P(IND, DP_REP),
            P(IND, DP_REP),
            P(IND),
            P(),
            P(),
        ),
        out_specs=(P(IND, DP_REP), P(IND), P()),
        check_vma=False,
    )
```

profile of v0, /device:TPU:1, one launch (start us, length us, event | category | flops | bytes accessed | tf_op | source)
XLA Modules:
  0.0 345.0 jit_solution(10306386077363218680)
XLA Ops:
  7.2 2.1 broadcast_in_dim.6
  9.3 6.7 %all-to-all-start = ((f32[4,1024,64]{1,2,0:T(8,128)}), f32[4,1024,64]{1,2,0:T(8,128)S(1)}, u32[]{:S(2)}, u32[]{:S(2)}) async-start(f32[4,1024,64]{1,2,0:T(8,128)} %broadcast_in_dim.6), calls=%async_computation | async-start | bytes 2097152 | tf_op jit(solution)/shard_map/all_to_all | solution.py:22
  16.0 1.3 fusion.15
  18.3 12.7 %all-to-all-done = f32[4,1024,64]{1,2,0:T(8,128)S(1)} async-done(((f32[4,1024,64]{1,2,0:T(8,128)}), f32[4,1024,64]{1,2,0:T(8,128)S(1)}, u32[]{:S(2)}, u32[]{:S(2)}) %all-to-all-start) | async-done | bytes 1048608 | tf_op jit(solution)/shard_map/all_to_all | solution.py:22
  32.0 13.6 %multiply_convert_fusion = bf16[4096,768]{1,0:T(8,128)(2,1)S(1)} fusion(f32[768]{0:T(1024)S(1)} %multiply_reduce_fusion.2, f32[4096]{0:T(1024)S(1)} %bitcast.44, f32[]{:T(128)} %bitcast, f32[4096,64]{0,1:T(8,128)S(1)} %bitcast.41, f32[64]{0:T(128)S(1)} %copy-done.7, bf16[768,64]{0,1:T(8,128)(2,1)S(1)} %copy-done.4), kind=kOutput, calls=%fused_computation | convolution fusion | flops 2435153920 | bytes 7458052 | tf_op jit(solution)/shard_map/dot_general | solution.py:69
  45.6 7.9 %multiply_reduce_fusion = (f32[768]{0:T(1024)S(1)}, bf16[768,1024]{1,0:T(8,128)(2,1)}) fusion(bf16[4096,768]{1,0:T(8,128)(2,1)S(1)} %multiply_convert_fusion, bf16[1024,4096]{1,0:T(8,128)(2,1)S(1)} %bitcast.46), kind=kOutput, calls=%fused_computation.2 | convolution fusion | flops 6445595648 | bytes 16256000 | tf_op jit(solution)/shard_map/dot_general | solution.py:91
  53.8 53.3 %all-gather.2.cloned.1.call-done = bf16[4096,768]{0,1:T(8,128)(2,1)} async-done(((bf16[1024,768]{0,1:T(8,128)(2,1)}), bf16[4096,768]{0,1:T(8,128)(2,1)}) %all-gather.2.cloned.1.call-update) | async-done | bytes 6291472 | tf_op jit(solution)/shard_map/all_gather | solution.py:97
  107.1 11.3 %convolution_convert_fusion = bf16[1024,4096]{1,0:T(8,128)(2,1)} fusion(bf16[768,1024]{1,0:T(8,128)(2,1)} %get-tuple-element.8, bf16[4096,768]{0,1:T(8,128)(2,1)} %all-gather.2.cloned.1.call-done), kind=kOutput, calls=%fused_computation.1 | convolution fusion | flops 6446645248 | bytes 16252928 | tf_op jit(solution)/shard_map/dot_general | solution.py:95
  118.4 11.9 %copy.27 = bf16[1024,4096]{0,1:T(8,128)(2,1)} copy(bf16[1024,4096]{1,0:T(8,128)(2,1)} %convolution_convert_fusion) | data formatting | bytes 16777216 | tf_op jit(solution)/shard_map/convert_element_type | solution.py:107
  130.3 8.4 %copy.28 = bf16[4,8,2,1024,64]{3,4,2,1,0:T(8,128)(2,1)} copy(bf16[4,8,2,1024,64]{3,4,0,2,1:T(8,128)(2,1)} %bitcast.38) | data formatting | bytes 16777216 | tf_op jit(solution)/shard_map/transpose | solution.py:44
  138.8 82.2 %reduce-scatter.4.cloned.1.call-done = bf16[16,1024,64]{1,2,0:T(8,128)(2,1)} async-done(((bf16[64,1024,64]{1,2,0:T(8,128)(2,1)}), bf16[16,1024,64]{1,2,0:T(8,128)(2,1)}) %reduce-scatter.4.cloned.1.call-update) | async-done | bytes 2097168 | tf_op jit(solution)/shard_map/reduce_scatter | solution.py:46
  221.1 1.3 convolution_reduce_fusion
  223.1 5.0 %all-to-all-start.1 = ((f32[4,1,1536]{2,1,0:T(1,128)}), f32[4,1,1536]{2,1,0:T(1,128)S(1)}, u32[]{:S(2)}, u32[]{:S(2)}) async-start(f32[4,1,1536]{2,1,0:T(1,128)} %broadcast_in_dim.7), calls=%async_computation.4 | async-start | bytes 49152 | tf_op jit(solution)/shard_map/all_to_all | solution.py:22
  228.1 33.8 %reduce-scatter.6.cloned.1.call-done = bf16[2,1024,64]{1,2,0:T(8,128)(2,1)} async-done(((bf16[16,1024,64]{1,2,0:T(8,128)(2,1)}), bf16[2,1024,64]{1,2,0:T(8,128)(2,1)}) %reduce-scatter.6.cloned.1.call-update) | async-done | bytes 262160 | tf_op jit(solution)/shard_map/reduce_scatter | solution.py:46
  262.7 1.2 fusion.9
  265.5 9.2 %all-to-all-start.2 = ((f32[64,1,1025]{2,1,0:T(1,128)}), f32[64,1,1025]{2,1,0:T(1,128)S(1)}, u32[]{:S(2)}, u32[]{:S(2)}) async-start(f32[64,1,1025]{2,1,0:T(1,128)} %broadcast_in_dim.8), calls=%async_computation.5 | async-start | bytes 589824 | tf_op jit(solution)/shard_map/all_to_all | solution.py:22
  276.0 9.2 %reduce-scatter.8.cloned.1.call-done = bf16[1,1024,64]{1,2,0:T(8,128)(2,1)} async-done(((bf16[2,1024,64]{1,2,0:T(8,128)(2,1)}), bf16[1,1024,64]{1,2,0:T(8,128)(2,1)}) %reduce-scatter.8.cloned.1.call-update) | async-done | bytes 131088 | tf_op jit(solution)/shard_map/reduce_scatter | solution.py:46
  285.2 3.0 fusion.5
  288.2 14.0 %psum.35 = f32[]{:T(128)} all-reduce(f32[]{:T(128)} %get-tuple-element.3), channel_id=1, replica_groups=mesh['dp_0'=8,'dp_1'=2,'rep'=4,'ind_0'=2,'ind_1'=2] {'dp_0'}, use_global_device_ids=true, to_apply=%region_10.0 | all-reduce | flops 1 | bytes 8 | tf_op jit(solution)/shard_map/psum | solution.py:61
  302.2 4.4 %psum.36 = f32[]{:T(128)} all-reduce(f32[]{:T(128)} %psum.35), channel_id=1, replica_groups=mesh['dp_0'=8,'dp_1'=2,'rep'=4,'ind_0'=2,'ind_1'=2] {'dp_1'}, use_global_device_ids=true, to_apply=%region_11.0 | all-reduce | flops 1 | bytes 8 | tf_op jit(solution)/shard_map/psum | solution.py:61
  306.8 9.5 %psum.37 = f32[]{:T(128)} all-reduce(f32[]{:T(128)} %psum.36), channel_id=1, replica_groups=mesh['dp_0'=8,'dp_1'=2,'rep'=4,'ind_0'=2,'ind_1'=2] {'rep'}, use_global_device_ids=true, to_apply=%region_12.0 | all-reduce | flops 1 | bytes 8 | tf_op jit(solution)/shard_map/psum | solution.py:61
  316.4 1.2 fusion.8
  317.6 6.0 %psum.38 = f32[]{:T(128)} all-reduce(f32[]{:T(128)} %psum.37), channel_id=1, replica_groups=mesh['dp_0'=8,'dp_1'=2,'rep'=4,'ind_0'=2,'ind_1'=2] {'ind_0'}, use_global_device_ids=true, to_apply=%region_13.0 | all-reduce | flops 1 | bytes 8 | tf_op jit(solution)/shard_map/psum | solution.py:61
  324.1 11.8 %psum.39 = f32[]{:T(128)} all-reduce(f32[]{:T(128)} %psum.38), channel_id=1, replica_groups=mesh['dp_0'=8,'dp_1'=2,'rep'=4,'ind_0'=2,'ind_1'=2] {'ind_1'}, use_global_device_ids=true, to_apply=%region_14.0 | all-reduce | flops 1 | bytes 8 | tf_op jit(solution)/shard_map/psum | solution.py:61
  (46 shorter events, 6.0 us)
Async XLA Ops:
  7.2 213.9 %copy-start = (f32[1024]{0:T(1024)S(1)}, f32[1024]{0:T(1024)}, u32[]{:S(2)}) copy-start(f32[1024]{0:T(1024)} %param.14) | copy-start | bytes 12292
  7.2 24.7 %copy-start.7 = (f32[64]{0:T(128)S(1)}, f32[64]{0:T(128)}, u32[]{:S(2)}) copy-start(f32[64]{0:T(128)} %param.18) | copy-start | bytes 772
  7.2 24.7 %copy-start.4 = (bf16[768,64]{0,1:T(8,128)(2,1)S(1)}, bf16[768,64]{0,1:T(8,128)(2,1)}, u32[]{:S(2)}) copy-start(bf16[768,64]{0,1:T(8,128)(2,1)} %param.10) | copy-start | bytes 294916
  9.3 21.7 %all-to-all-start = ((f32[4,1024,64]{1,2,0:T(8,128)}), f32[4,1024,64]{1,2,0:T(8,128)S(1)}, u32[]{:S(2)}, u32[]{:S(2)}) async-start(f32[4,1024,64]{1,2,0:T(8,128)} %broadcast_in_dim.6), calls=%async_computation | async-start | bytes 2097152 | tf_op jit(solution)/shard_map/all_to_all | solution.py:22
  16.0 91.1 %all-gather.2.cloned.1.call-start = ((), (), s32[]{:S(2)}) async-start(), calls=%async_computation.6 | async-start | bytes 7864320 | tf_op jit(solution)/shard_map/all_gather | solution.py:97
  31.8 13.7 %slice-start = ((s8[8388608]{0:T(1024)(128)(4,1)}), s8[4194304]{0:T(1024)(128)(4,1)S(1)}, s32[]{:S(2)}) async-start(s8[8388608]{0:T(1024)(128)(4,1)} %bitcast.45), calls=%async_computation.10 | async-start | bytes 8388608
  31.9 13.6 %slice-start.1 = ((s8[8388608]{0:T(1024)(128)(4,1)}), s8[4194304]{0:T(1024)(128)(4,1)S(1)}, s32[]{:S(2)}) async-start(s8[8388608]{0:T(1024)(128)(4,1)} %bitcast.45), calls=%async_computation.11 | async-start | bytes 8388608
  53.6 167.5 %reduce-scatter.4.cloned.1.call-start = ((), (), s32[]{:S(2)}) async-start(), calls=%async_computation.7 | async-start | bytes 10485760 | tf_op jit(solution)/shard_map/reduce_scatter | solution.py:46
  138.7 82.3 %copy-start.5 = (f32[768]{0:T(1024)S(1)}, f32[768]{0:T(1024)}, u32[]{:S(2)}) copy-start(f32[768]{0:T(1024)} %param.11) | copy-start | bytes 9220
  138.7 82.4 %copy-start.1 = (bf16[768,1024]{1,0:T(8,128)(2,1)S(1)}, bf16[768,1024]{1,0:T(8,128)(2,1)}, u32[]{:S(2)}) copy-start(bf16[768,1024]{1,0:T(8,128)(2,1)} %get-tuple-element.8) | copy-start | bytes 4718596
  138.7 146.5 %copy-start.2 = (f32[1024,64]{0,1:T(8,128)S(1)}, f32[1024,64]{0,1:T(8,128)}, u32[]{:S(2)}) copy-start(f32[1024,64]{0,1:T(8,128)} %param.15) | copy-start | bytes 786436
  138.7 146.5 %copy-start.3 = (f32[1024,64]{0,1:T(8,128)S(1)}, f32[1024,64]{0,1:T(8,128)}, u32[]{:S(2)}) copy-start(f32[1024,64]{0,1:T(8,128)} %param.16) | copy-start | bytes 786436
  138.7 177.6 %copy-start.6 = (f32[1024]{0:T(1024)S(1)}, f32[1024]{0:T(1024)}, u32[]{:S(2)}) copy-start(f32[1024]{0:T(1024)} %param.17) | copy-start | bytes 12292
  138.8 123.1 %reduce-scatter.6.cloned.1.call-start = ((), (), s32[]{:S(2)}) async-start(), calls=%async_computation.8 | async-start | bytes 2359296 | tf_op jit(solution)/shard_map/reduce_scatter | solution.py:46
  223.1 39.6 %all-to-all-start.1 = ((f32[4,1,1536]{2,1,0:T(1,128)}), f32[4,1,1536]{2,1,0:T(1,128)S(1)}, u32[]{:S(2)}, u32[]{:S(2)}) async-start(f32[4,1,1536]{2,1,0:T(1,128)} %broadcast_in_dim.7), calls=%async_computation.4 | async-start | bytes 49152 | tf_op jit(solution)/shard_map/all_to_all | solution.py:22
  228.1 57.1 %reduce-scatter.8.cloned.1.call-start = ((), (), s32[]{:S(2)}) async-start(), calls=%async_computation.9 | async-start | bytes 393216 | tf_op jit(solution)/shard_map/reduce_scatter | solution.py:46
  265.5 41.2 %all-to-all-start.2 = ((f32[64,1,1025]{2,1,0:T(1,128)}), f32[64,1,1025]{2,1,0:T(1,128)S(1)}, u32[]{:S(2)}, u32[]{:S(2)}) async-start(f32[64,1,1025]{2,1,0:T(1,128)} %broadcast_in_dim.8), calls=%async_computation.5 | async-start | bytes 589824 | tf_op jit(solution)/shard_map/all_to_all | solution.py:22
Sparse Core Ops, SparseCore 0:
  53.7 53.3 all-gather.1
  138.9 82.1 reduce-scatter.3
  223.6 38.2 reduce-scatter.5
  264.2 20.9 reduce-scatter.7
where the time goes:
time: 346 us; the launch traced here: 345 us
  waiting for transfers between devices  191 us (55%)
  blocking collectives  45.7 us (13%)
  matrix products  34.9 us (10%)
  local copies, waits for them, and re-layouts  25.9 us (7%)
  starting transfers between devices  21.1 us (6%)
  between operations  17.8 us (5%)
  other arithmetic  8.27 us (2%)
    reduce_scatter x3, waiting for transfers between devices, sum_in_order(): blocks = lax.psum_scatter(blocks, axes[k], scatter_dimension=0, tiled=True)  125 us
    all_gather x1, waiting for transfers between devices, shards(): lax.all_gather(white, IND, axis=0, tiled=True)  53.3 us
    psum x5, blocking collectives, one_axis_at_a_time(): return functools.reduce(lax.psum, axes, array)  45.7 us
    all_to_all x3, starting transfers between devices, sent_to_all(): return lax.all_to_all(copies, axis, split_axis=0, concat_axis=0, tiled=True)  20.8 us
    dot_general x1, matrix products, cross_cov(): inner = jnp.dot(scaled_z, scaled_x.T, precision=lax.Precision.HIGHEST)  13.6 us
    all_to_all x3, waiting for transfers between devices, sent_to_all(): return lax.all_to_all(copies, axis, split_axis=0, concat_axis=0, tiled=True)  12.7 us
    convert_element_type x1, local copies, waits for them, and re-layouts, shards(): gram_part.astype(jnp.bfloat16)  11.9 us
    dot_general x1, matrix products, shards(): lax.dot_general(white, lax.all_gather(white, IND, axis=0, tiled=True), ((...  11.3 us
  transfers between devices with their start and end apart: 7, of which 5 were waited for; matrix products, arithmetic and copies ran while one was open for 3% of the time, Pallas kernels for 0%

commit v1 on v0

v1 whole, which is shorter than its diff:
```python
import jax
import jax.numpy as jnp
from jax import lax
from jax.experimental import pallas as pl
from jax.experimental.pallas import tpu as pltpu
from jax.sharding import Mesh
from jax.sharding import PartitionSpec as P

AXES = ("dp_0", "dp_1", "rep", "ind_0", "ind_1")
IND = ("ind_0", "ind_1")
DP_REP = ("dp_0", "dp_1", "rep")
MESH = pl.DeviceIdType.MESH
VMEM = pl.BlockSpec(memory_space=pltpu.VMEM)
ANY = pl.BlockSpec(memory_space=pl.ANY)
F32 = jnp.float32
BF16 = jnp.bfloat16
ROUNDS = 10


def place():
    return tuple(lax.axis_index(a) for a in AXES)


def remote(src, dst, send, recv, to):
    return pltpu.make_async_remote_copy(
        src_ref=src, dst_ref=dst, send_sem=send, recv_sem=recv, device_id=to, device_id_type=MESH
    )


def share_kernel(z_ref, p_ref, t_ref, allz, p_out, t_out, send, recv, local):
    z, lo, y, hi, core = place()
    mine = hi * 2 + core
    other = (1 - hi) * 2 + core
    partner = (z, lo, y, hi, 1 - core)
    across = (z, 1 - lo, y, 1 - hi, core)
    swap = (z, 1 - lo, y, hi, core)
    over = remote(z_ref, allz.at[mine], send.at[0], recv.at[0], across)
    over.start()

    @pl.when(hi == 0)
    def _():
        remote(p_ref, p_out, send.at[3], recv.at[3], swap).start()
        remote(t_ref, t_out, send.at[4], recv.at[4], swap).start()

    near = remote(z_ref, allz.at[mine], send.at[1], recv.at[1], partner)
    near.start()
    own = pltpu.make_async_copy(z_ref, allz.at[mine], local)
    own.start()

    @pl.when(hi == 1)
    def _():
        p_out[...] = p_ref[...]
        t_out[...] = t_ref[...]

    over.wait_recv()
    on = remote(allz.at[other], allz.at[other], send.at[2], recv.at[2], partner)
    on.start()
    own.wait()
    near.wait_recv()
    on.wait_recv()

    @pl.when(hi == 0)
    def _():
        remote(p_ref, p_out, send.at[3], recv.at[3], swap).wait()
        remote(t_ref, t_out, send.at[4], recv.at[4], swap).wait()

    over.wait_send()
    near.wait_send()
    on.wait_send()


def share(z_t, p_t, tgt):
    return pl.pallas_call(
        share_kernel,
        out_shape=(
            jax.ShapeDtypeStruct((4, *z_t.shape), F32),
            jax.ShapeDtypeStruct(p_t.shape, BF16),
            jax.ShapeDtypeStruct(tgt.shape, F32),
        ),
        in_specs=[VMEM] * 3,
        out_specs=(VMEM, VMEM, VMEM),
        scratch_shapes=[
            pltpu.SemaphoreType.DMA((5,)),
            pltpu.SemaphoreType.DMA((5,)),
            pltpu.SemaphoreType.DMA,
        ],
        compiler_params=pltpu.CompilerParams(has_side_effects=True),
        name="share",
    )(z_t, p_t, tgt)


def round_of(t):
    late = jnp.minimum(t // 2, 1)
    is_b = (t % 2) * late
    a = t * (1 - late) + (1 + t // 2) * late
    is_h = (1 - is_b) * (a // 4)
    g = is_b * (t // 2 - 1) + (1 - is_b) * (a - 4 * is_h)
    return is_b, is_h, g


def gram_kernel(
    white, pm_ref, out, pm_out,
    wbuf, pay, y1, y2, zs, zr, xk, xs, xr, fin, fint, own, pmr,
    g_s, g_r, p_s, p_r, y1_s, y1_r, y2_s, y2_r, z_s, z_r, x_s, x_r, pm_s, pm_r, f_s, own_sem, w_sem,
):
    z, lo, y, hi, core = place()
    mine = hi * 2 + core
    yp, ym, y2p = (y + 1) % 4, (y + 3) % 4, (y + 2) % 4
    partner = (z, lo, y, hi, 1 - core)
    gather_to = (z, 1 - lo, y, 1 - hi, (core + 1 - hi) % 2)

    load = pltpu.make_async_copy(white, wbuf.at[core], w_sem)
    load.start()
    pm_to = (partner, (z, 1 - lo, y, 1 - hi, core), (z, 1 - lo, y, 1 - hi, 1 - core))
    pm_copies = [remote(pm_ref, pmr.at[k], pm_s.at[k], pm_r.at[k], to) for k, to in enumerate(pm_to)]
    for c in pm_copies:
        c.start()
    load.wait()

    def gather_piece(g, k):
        rows = pl.ds(pl.multiple_of(k * 128 + 32 * g, 32), 32)
        return remote(wbuf.at[core, rows], wbuf.at[2, rows], g_s.at[g], g_r.at[g], gather_to)

    def gather_start(g, _):
        lax.fori_loop(0, 8, lambda k, c: (gather_piece(g, k).start(), c)[1], 0)
        return 0

    lax.fori_loop(0, 4, gather_start, 0)
    to_partner = remote(wbuf.at[core], wbuf.at[core], p_s, p_r, partner)
    to_partner.start()

    def gather_all(g):
        rows = pl.ds(0, 256)
        return remote(wbuf.at[core, rows], wbuf.at[2, rows], g_s.at[g], g_r.at[g], gather_to)

    def y1_copies(t):
        up = pl.ds(pl.multiple_of(y2p * 64, 64), 32)
        down = pl.ds(pl.multiple_of(y2p * 64 + 32, 32), 32)
        return (
            remote(pay.at[t, up], y1.at[t, 0], y1_s.at[t, 0], y1_r.at[t, 0], (z, lo, yp, hi, core)),
            remote(pay.at[t, down], y1.at[t, 1], y1_s.at[t, 1], y1_r.at[t, 1], (z, lo, ym, hi, core)),
        )

    def y2_copies(t):
        up = pl.ds(pl.multiple_of(yp * 64, 64), 64)
        down = pl.ds(pl.multiple_of(ym * 64, 64), 64)
        return (
            remote(pay.at[t, up], y2.at[t, 0], y2_s.at[t, 0], y2_r.at[t, 0], (z, lo, yp, hi, core)),
            remote(pay.at[t, down], y2.at[t, 1], y2_s.at[t, 1], y2_r.at[t, 1], (z, lo, ym, hi, core)),
        )

    def z_copy(t, d):
        to = (z + d) % 8
        cols = pl.ds(pl.multiple_of(to * 128, 128), 128)
        return remote(zs.at[t, :, cols], zr.at[t, d - 1], z_s.at[t], z_r.at[t], (to, lo, y, hi, core))

    def z_all(t):
        return remote(zr.at[t], zr.at[t], z_s.at[t], z_r.at[t], ((z + 1) % 8, lo, y, hi, core))

    def x_copy(t):
        return remote(xs.at[t], xr.at[t], x_s.at[t], x_r.at[t], (z, 1 - lo, y, hi, core))

    def compute(t):
        is_b, is_h, g = round_of(t)
        plain = 1 - is_h

        @pl.when(is_b == 1)
        def _():
            gather_all(g).wait_recv()

        @pl.when(is_h * (1 - g) == 1)
        def _():
            to_partner.wait_recv()

        left = is_b * 2 + is_h + plain * (1 - is_b) * core
        right = plain * core
        shift = g + is_h * 2 * core
        a = jnp.concatenate(
            [wbuf[left, pl.ds(pl.multiple_of(k * 128 + 32 * shift, 32), 32), :] for k in range(8)], axis=0
        )
        for j in range(4):
            b = wbuf[right, j * 256 : (j + 1) * 256, :]
            part = lax.dot_general(a, b, (((1,), (1,)), ((), ())), preferred_element_type=F32)
            pay[t, :, j * 256 : (j + 1) * 256] = part.astype(BF16)
        for c in y1_copies(t):
            c.start()

    def after_y1(t):
        for k, c in enumerate(y1_copies(t)):
            c.wait_recv()
            rows = pl.ds(pl.multiple_of((yp, ym)[k] * 64 + 32 * k, 32), 32)
            pay[t, rows, :] = (pay[t, rows, :].astype(F32) + y1[t, k].astype(F32)).astype(BF16)
        for c in y2_copies(t):
            c.start()

    def after_y2(t):
        for c in y2_copies(t):
            c.wait_recv()
        rows = pl.ds(pl.multiple_of(y * 64, 64), 64)
        total = pay[t, rows, :].astype(F32) + y2[t, 0].astype(F32) + y2[t, 1].astype(F32)
        zs[t] = total.astype(BF16)
        for d in range(1, 8):
            z_copy(t, d).start()

    def after_z(t):
        z_all(t).wait_recv()
        total = zs[t, :, pl.ds(pl.multiple_of(z * 128, 128), 128)].astype(F32)
        for d in range(7):
            total = total + zr[t, d].astype(F32)
        xk[t] = total

        xs[t] = xk[t, pl.ds(pl.multiple_of((1 - lo) * 32, 32), 32), :].astype(BF16)
        x_copy(t).start()

    def after_x(t):
        x_copy(t).wait_recv()
        is_b, is_h, g = round_of(t)
        total = xk[t, pl.ds(pl.multiple_of(lo * 32, 32), 32), :] + xr[t].astype(F32)
        slot = is_b + 2 * is_h
        row = g * 32 + is_h * core * 64
        fin[slot, pl.ds(pl.multiple_of(row, 32), 32), :] = total.astype(BF16)

    zero = jnp.zeros((128, 128), BF16)
    fin[2] = zero

    def step(t, carry):
        for lag, work in ((4, after_x), (3, after_z), (2, after_y2), (1, after_y1), (0, compute)):

            @pl.when((t >= lag) & (t < ROUNDS + lag))
            def _(lag=lag, work=work):
                work(t - lag)

        return carry

    lax.fori_loop(0, ROUNDS + 4, step, 0)

    fint[0] = fin[1].astype(F32).T.astype(BF16)
    fint[1] = fin[2].astype(F32).T.astype(BF16)

    nxt = (1 - hi) * 2 + (core + hi) % 2
    low, high = hi * 2, hi * 2 + 1
    me = (((z * 2 + lo) * 4 + y) * 2 + hi) * 2 + core
    direct = pl.ds(pl.multiple_of(z * 128, 128), 128)
    mirror = pl.ds(pl.multiple_of(256 * y + 128 * lo, 128), 128)

    def owner(q, ind):
        return (q // 8, (q // 4) % 2, q % 4, ind // 2, ind % 2)

    sends = []
    for e in range(2):
        rows = slice(64 * e, 64 * e + 64)
        sends.append((fin.at[0, rows], own.at[0, :, direct], own_sem.at[0], owner(16 * mine + 4 * y + 2 * lo + e, mine)))
        sends.append((fin.at[1, rows], own.at[0, :, direct], own_sem.at[0], owner(16 * nxt + 4 * y + 2 * lo + e, mine)))
        sends.append((fint.at[0, rows], own.at[0, :, mirror], own_sem.at[0], owner(16 * mine + 2 * z + e, nxt)))
        sends.append((fint.at[1, rows], own.at[core, :, mirror], own_sem.at[core], owner(16 * low + 2 * z + e, high)))
    half = pl.ds(pl.multiple_of(64 * core, 64), 64)
    sends.append((fin.at[2, half], own.at[0, :, direct], own_sem.at[0], owner(16 * high + 4 * y + 2 * lo + core, low)))

    def flat(d):
        return (((d[0] * 2 + d[1]) * 4 + d[2]) * 2 + d[3]) * 2 + d[4]

    for k, (src, dst, sem, to) in enumerate(sends):

        @pl.when(flat(to) != me)
        def _(k=k, src=src, dst=dst, sem=sem, to=to):
            remote(src, dst, f_s.at[k], sem, to).start()

        @pl.when(flat(to) == me)
        def _(src=src, dst=dst, sem=sem):
            pltpu.make_async_copy(src, dst, sem).start()

    for c in pm_copies:
        c.wait_recv()
    pm_out[...] = pm_ref[...] + pmr[0] + pmr[1] + pmr[2]

    pltpu.make_async_copy(own.at[0], own.at[0], own_sem.at[0]).wait()
    both = core * (1 - jnp.minimum(jnp.abs(z // 2 - low), 1))

    @pl.when(both == 0)
    def _():
        out[...] = own[0]

    @pl.when(both == 1)
    def _():
        pltpu.make_async_copy(own.at[1], own.at[1], own_sem.at[1]).wait()
        out[...] = own[0] + own[1]

    for k, (src, dst, sem, to) in enumerate(sends):

        @pl.when(flat(to) != me)
        def _(k=k, src=src, dst=dst, sem=sem, to=to):
            remote(src, dst, f_s.at[k], sem, to).wait_send()

    for c in pm_copies:
        c.wait_send()
    to_partner.wait_send()

    def drain(t, carry):
        for c in y1_copies(t) + y2_copies(t):
            c.wait_send()
        z_all(t).wait_send()
        x_copy(t).wait_send()
        return carry

    lax.fori_loop(0, ROUNDS, drain, 0)
    lax.fori_loop(0, 4, lambda g, c: (gather_all(g).wait_send(), c)[1], 0)


def gram_reduced(white, pm):
    dma = pltpu.SemaphoreType.DMA
    n = white.shape[1]
    return pl.pallas_call(
        gram_kernel,
        out_shape=(jax.ShapeDtypeStruct((64, 1024), BF16), jax.ShapeDtypeStruct((8, 128), F32)),
        in_specs=[ANY, VMEM],
        out_specs=(VMEM, VMEM),
        scratch_shapes=[
            pltpu.VMEM((3, 1024, n), BF16),
            pltpu.VMEM((ROUNDS, 256, 1024), BF16),
            pltpu.VMEM((ROUNDS, 2, 32, 1024), BF16),
            pltpu.VMEM((ROUNDS, 2, 64, 1024), BF16),
            pltpu.VMEM((ROUNDS, 64, 1024), BF16),
            pltpu.VMEM((ROUNDS, 7, 64, 128), BF16),
            pltpu.VMEM((ROUNDS, 64, 128), F32),
            pltpu.VMEM((ROUNDS, 32, 128), BF16),
            pltpu.VMEM((ROUNDS, 32, 128), BF16),
            pltpu.VMEM((3, 128, 128), BF16),
            pltpu.VMEM((2, 128, 128), BF16),
            pltpu.VMEM((2, 64, 1024), BF16),
            pltpu.VMEM((3, 8, 128), F32),
            dma((4,)), dma((4,)), dma, dma,
            dma((ROUNDS, 2)), dma((ROUNDS, 2)), dma((ROUNDS, 2)), dma((ROUNDS, 2)),
            dma((ROUNDS,)), dma((ROUNDS,)), dma((ROUNDS,)), dma((ROUNDS,)),
            dma((3,)), dma((3,)), dma((9,)), dma((2,)), dma,
        ],
        compiler_params=pltpu.CompilerParams(has_side_effects=True, vmem_limit_bytes=40 * 2**20),
        name="gram_reduced",
    )(white, pm)


def three_parts(v):
    a = lax.reduce_precision(v, 8, 7)
    b = lax.reduce_precision(v - a, 8, 7)
    return a.astype(BF16), b.astype(BF16), (v - a - b).astype(BF16)


def shards(points, targets, inducing, whitening, mean_v, covariance, precision, natural_one, lengthscales, hypers):
    signal, noise_var = hypers[0], hypers[1]
    own_rows, own_points = inducing.shape[0], points.shape[0]
    tgt = jnp.pad(targets, (0, 1024 - own_points)).reshape(8, 128)
    all_z, pts, tgt = share(inducing.T, points.T, tgt)
    tgt_row = tgt.reshape(-1)[:own_points]
    scale = lengthscales[:, None]
    norm_x = jnp.sum(jnp.square(pts.astype(F32) / scale), axis=0)
    norm_z = jnp.sum(jnp.square(all_z / scale), axis=1).reshape(-1)
    parts = jnp.concatenate(three_parts(all_z / (scale * scale)), axis=1)
    inner = lax.dot_general(
        parts, jnp.concatenate([pts] * 3, axis=0), (((1,), (0,)), ((), ())), preferred_element_type=F32
    ).reshape(-1, own_points)
    cross = (signal * jnp.exp(-0.5 * (norm_z[:, None] + norm_x[None, :] - 2.0 * inner))).astype(BF16)
    white = jnp.dot(whitening, cross, preferred_element_type=F32).astype(BF16)
    wide = white.astype(F32)
    pm = jnp.sum(mean_v[:, None] * wide, axis=0)
    proj = jnp.sum(wide * tgt_row[None, :], axis=1)
    square = jnp.sum(wide * wide)
    gram_t, pm = gram_reduced(white, jnp.pad(pm, (0, 1024 - own_points)).reshape(8, 128))
    gram_t = gram_t.astype(F32)
    trace = jnp.sum(covariance.T * gram_t)
    fit = 0.25 * (jnp.sum(jnp.square(tgt - pm)) + signal * own_points) - square
    mine = lax.axis_index(IND)
    slots = jnp.where(jnp.arange(4)[:, None] == mine, proj[None, :], 0.0).reshape(-1)
    total = lax.psum(jnp.concatenate([slots, (trace + fit)[None]]), AXES)
    proj = lax.dynamic_slice(total, (mine * own_rows,), (own_rows,))
    count = own_points * lax.axis_size(DP_REP)
    expected_fit = -0.5 * jnp.log(2.0 * jnp.pi * noise_var) - total[-1] / (2.0 * noise_var * count)
    row_ids = mine * own_rows + jnp.arange(own_rows, dtype=jnp.int32)
    col_ids = lax.axis_index(DP_REP) * 64 + jnp.arange(64, dtype=jnp.int32)
    identity = (row_ids[None, :] == col_ids[:, None]).astype(F32)
    precision_new = (0.5 * precision.T + 0.5 * (identity + gram_t / noise_var)).T
    natural_new = 0.5 * natural_one + 0.5 * proj / noise_var
    return precision_new, natural_new, expected_fit


def solution(mesh):
    finer = Mesh(mesh.devices.reshape(8, 2, mesh.shape["rep"], 2, 2), AXES)
    return jax.shard_map(
        shards,
        mesh=finer,
        in_specs=(
            P(DP_REP, None), P(DP_REP), P(IND, None), P(IND, None), P(IND),
            P(IND, DP_REP), P(IND, DP_REP), P(IND), P(), P(),
        ),
        out_specs=(P(IND, DP_REP), P(IND), P()),
        check_vma=False,
    )
```

time: 346 us -> 232 us (0.67)
  waiting for transfers between devices: 191 us -> 0 us
  Pallas kernels: 0 us -> 125 us
  blocking collectives: 45.7 us -> 75.8 us
  matrix products: 34.9 us -> 10.7 us
  local copies, waits for them, and re-layouts: 25.9 us -> 2.53 us
  starting transfers between devices: 21.1 us -> 0 us
  between operations: 17.8 us -> 6.69 us
    reduce_scatter x3 -> x0, waiting for transfers between devices: 125 us -> none  [sum_in_order(): blocks = lax.psum_scatter(blocks, axes[k], scatter_dimension=0, tiled=True)]
    pallas_call x0 -> x2, Pallas kernels: none -> 125 us  [the longest x1 98.1 us: gram_reduced(): pl.pallas_call(gram_kernel, out_shape=(jax.ShapeDtypeStruct((64, 1024), B...]
    all_gather x1 -> x0, waiting for transfers between devices: 53.3 us -> none  [shards(): lax.all_gather(white, IND, axis=0, tiled=True)]
    psum x5 -> x1, blocking collectives: 45.7 us -> 75.8 us  [shards(): total = lax.psum(jnp.concatenate([slots, (trace + fit)[None]]), AXES)]
    dot_general x5 -> x2, matrix products: 34.9 us -> 10.7 us  [the longest x1 7.71 us: shards(): white = jnp.dot(whitening, cross, preferred_element_type=F32).astype(BF16)]
    all_to_all x3 -> x0, starting transfers between devices: 20.8 us -> none  [sent_to_all(): return lax.all_to_all(copies, axis, split_axis=0, concat_axis=0, tiled=True)]
    all_to_all x3 -> x0, waiting for transfers between devices: 12.7 us -> none  [sent_to_all(): return lax.all_to_all(copies, axis, split_axis=0, concat_axis=0, tiled=True)]
    convert_element_type x1 -> x0, local copies, waits for them, and re-layouts: 11.9 us -> none  [shards(): gram_part.astype(jnp.bfloat16)]
  transfers between devices with their start and end apart: 7 -> 0, of which waited for: 5 -> 0; matrix products, arithmetic and copies ran while one was open for 3% -> 0% of each run, Pallas kernels for 0% -> 0%
where the time goes in v1:
time: 232 us
  Pallas kernels  125 us (54%)
  blocking collectives  75.8 us (33%)
  other arithmetic  10.9 us (5%)
  matrix products  10.7 us (5%)
  between operations  6.69 us (3%)
  local copies, waits for them, and re-layouts  2.53 us (1%)
    pallas_call x1, Pallas kernels, gram_reduced(): pl.pallas_call(gram_kernel, out_shape=(jax.ShapeDtypeStruct((64, 1024), B...  98.1 us
    psum x1, blocking collectives, shards(): total = lax.psum(jnp.concatenate([slots, (trace + fit)[None]]), AXES)  75.8 us
    pallas_call x1, Pallas kernels, share(): pl.pallas_call(share_kernel, out_shape=(jax.ShapeDtypeStruct((4, *z_t.sha...  26.8 us
    dot_general x1, matrix products, shards(): white = jnp.dot(whitening, cross, preferred_element_type=F32).astype(BF16)  7.71 us

profile of v1, /device:TPU:1, one launch (start us, length us, event | category | flops | bytes accessed | tf_op | source)
XLA Modules:
  0.0 231.5 jit_solution(9076343458205863710)
XLA Ops:
  0.6 1.3 pad_bitcast_fusion.1.t_ref
  1.9 26.8 %share.1 = (f32[4,64,1024]{2,1,0:T(8,128)}, bf16[64,768]{1,0:T(8,128)(2,1)}, f32[8,128]{1,0:T(8,128)}) custom-call(f32[64,1024]{1,0:T(8,128)} %bitcast.44, bf16[64,768]{1,0:T(8,128)(2,1)} %bitcast.45, f32[8,128]{1,0:T(8,128)} %pad_bitcast_fusion.1.t_ref), custom_call_target="tpu_custom_call" | custom-call | tf_op jit(solution)/shard_map/share/pallas_call | solution.py:73
  28.7 0.7 mul.91
  29.4 1.7 reduce-precision_convert_fusion.1
  31.1 0.0 copy-start.5
  31.2 0.0 copy-start.6
  31.2 0.0 slice-start
  31.2 3.0 %broadcast_multiply_fusion = f32[4,1024,768]{2,1,0:T(8,128)S(1)} fusion(bf16[4,64,1024]{2,1,0:T(8,128)(2,1)S(1)} %get-tuple-element.18, bf16[4,64,1024]{2,1,0:T(8,128)(2,1)S(1)} %get-tuple-element.17, bf16[4,64,1024]{2,1,0:T(8,128)(2,1)S(1)} %get-tuple-element.16, bf16[64,768]{1,0:T(8,128)(2,1)} %get-tuple-element.9), kind=kOutput, calls=%fused_computation.5 | convolution fusion | flops 1216708608 | bytes 14254080 | tf_op jit(solution)/shard_map/dot_general | solution.py:357
  34.2 0.0 copy-done
  34.2 0.0 copy-done.5
  34.2 0.1 multiply_reduce_fusion.1
  34.3 0.7 fusion.24
  35.0 4.2 %fusion.3 = bf16[4096,768]{1,0:T(8,128)(2,1)S(1)} fusion(f32[4,1024,768]{2,1,0:T(8,128)S(1)} %broadcast_multiply_fusion, f32[768]{0:T(1024)S(1)} %multiply_reduce_fusion.1, f32[4096]{0:T(1024)S(1)} %bitcast.48, f32[]{:T(128)} %bitcast.1), kind=kLoop, calls=%fused_computation.4 | loop fusion | flops 15728640 | bytes 18893828 | tf_op jit(solution)/shard_map/convert_element_type | solution.py:360
  39.3 0.0 copy-start.1
  39.3 0.0 copy-start.2
  39.3 0.0 copy-start.4
  39.3 7.7 %fusion.5 = (f32[1024]{0:T(1024)S(1)}, f32[]{:T(128)}, f32[768]{0:T(1024)S(1)}, bf16[1024,768]{1,0:T(8,128)(2,1)S(1)}) fusion(f32[768]{0:T(1024)S(1)} %slice_bitcast_fusion, f32[1024]{0:T(1024)S(1)} %copy-done.7, bf16[1024,4096]{1,0:T(8,128)(2,1)S(1)} %bitcast.50, bf16[4096,768]{1,0:T(8,128)(2,1)S(1)} %fusion.3), kind=kOutput, calls=%fused_computation.10 | convolution fusion | flops 6448740352 | bytes 16267268 | tf_op jit(solution)/shard_map/dot_general | solution.py:361
  47.0 98.1 %gram_reduced.1 = (bf16[64,1024]{1,0:T(8,128)(2,1)S(1)}, f32[8,128]{1,0:T(8,128)S(1)}) custom-call(bf16[1024,768]{1,0:T(8,128)(2,1)S(1)} %get-tuple-element.24.white, f32[8,128]{1,0:T(8,128)S(1)} %pad_bitcast_fusion.pm_ref), custom_call_target="tpu_custom_call" | custom-call | tf_op jit(solution)/shard_map/gram_reduced/pallas_call | solution.py:312
  145.1 0.6 multiply_reduce_fusion.2
  147.7 2.1 fusion.22
  150.5 0.1 select_bitcast_fusion
  150.6 75.8 %psum.7 = f32[4097]{0:T(1024)S(1)} all-reduce(f32[4097]{0:T(1024)S(1)} %pad_maximum_fusion), channel_id=1, replica_groups=mesh['dp_0'=8,'dp_1'=2,'rep'=4,'ind_0'=2,'ind_1'=2] {'dp_0','dp_1','rep'..., use_global_device_ids=true, to_apply=%region_7.8 | all-reduce | flops 4097 | bytes 32776 | tf_op jit(solution)/shard_map/psum | solution.py:372
  226.4 0.5 slice.17
  229.0 1.4 divide_add_fusion
  (21 shorter events, 0.1 us)
Async XLA Ops:
  31.1 3.1 %copy-start = (bf16[64,768]{1,0:T(8,128)(2,1)S(1)}, bf16[64,768]{1,0:T(8,128)(2,1)}, u32[]{:S(2)}) copy-start(bf16[64,768]{1,0:T(8,128)(2,1)} %get-tuple-element.9) | copy-start | bytes 294916
  31.1 3.1 %copy-start.5 = (f32[64]{0:T(128)S(1)}, f32[64]{0:T(128)}, u32[]{:S(2)}) copy-start(f32[64]{0:T(128)} %param.18) | copy-start | bytes 772
  31.2 3.2 %copy-start.6 = (f32[2]{0:T(128)S(1)}, f32[2]{0:T(128)}, u32[]{:S(2)}) copy-start(f32[2]{0:T(128)} %param.19) | copy-start | bytes 28
  31.2 8.1 %slice-start = ((s8[8388608]{0:T(1024)(128)(4,1)}), s8[4194304]{0:T(1024)(128)(4,1)S(1)}, s32[]{:S(2)}) async-start(s8[8388608]{0:T(1024)(128)(4,1)} %bitcast.49), calls=%async_computation | async-start | bytes 8388608
  35.0 4.2 %copy-start.3 = (f32[8,128]{1,0:T(8,128)S(1)}, f32[8,128]{1,0:T(8,128)}, u32[]{:S(2)}) copy-start(f32[8,128]{1,0:T(8,128)} %get-tuple-element.11) | copy-start | bytes 12292
  35.0 4.2 %slice-start.1 = ((s8[8388608]{0:T(1024)(128)(4,1)}), s8[4194304]{0:T(1024)(128)(4,1)S(1)}, s32[]{:S(2)}) async-start(s8[8388608]{0:T(1024)(128)(4,1)} %bitcast.49), calls=%async_computation.1 | async-start | bytes 8388608
  35.0 4.2 %copy-start.7 = (f32[1024]{0:T(1024)S(1)}, f32[1024]{0:T(1024)}, u32[]{:S(2)}) copy-start(f32[1024]{0:T(1024)} %param.14) | copy-start | bytes 12292
  39.3 108.5 %copy-start.1 = (f32[1024,64]{0,1:T(8,128)S(1)}, f32[1024,64]{0,1:T(8,128)}, u32[]{:S(2)}) copy-start(f32[1024,64]{0,1:T(8,128)} %param.15) | copy-start | bytes 786436
  39.3 108.5 %copy-start.2 = (f32[1024,64]{0,1:T(8,128)S(1)}, f32[1024,64]{0,1:T(8,128)}, u32[]{:S(2)}) copy-start(f32[1024,64]{0,1:T(8,128)} %param.16) | copy-start | bytes 786436
  39.3 189.7 %copy-start.4 = (f32[1024]{0:T(1024)S(1)}, f32[1024]{0:T(1024)}, u32[]{:S(2)}) copy-start(f32[1024]{0:T(1024)} %param.17) | copy-start | bytes 12292

commit v2 on v1

--- a/solution.py
+++ b/solution.py
@@ -14,7 +14,7 @@
 ANY = pl.BlockSpec(memory_space=pl.ANY)
 F32 = jnp.float32
 BF16 = jnp.bfloat16
-ROUNDS = 10
+ROUNDS = 5
 
 
 def place():
@@ -25,6 +25,13 @@
     return pltpu.make_async_remote_copy(
         src_ref=src, dst_ref=dst, send_sem=send, recv_sem=recv, device_id=to, device_id_type=MESH
     )
+
+
+def greet(peers):
+    barrier = pltpu.get_barrier_semaphore()
+    for to in peers:
+        pl.semaphore_signal(barrier, inc=1, device_id=to, device_id_type=MESH)
+    pl.semaphore_wait(barrier, len(peers))
 
 
 def share_kernel(z_ref, p_ref, t_ref, allz, p_out, t_out, send, recv, local):
@@ -34,6 +41,7 @@
     partner = (z, lo, y, hi, 1 - core)
     across = (z, 1 - lo, y, 1 - hi, core)
     swap = (z, 1 - lo, y, hi, core)
+    greet((partner, across, swap))
     over = remote(z_ref, allz.at[mine], send.at[0], recv.at[0], across)
     over.start()
 
@@ -84,24 +92,23 @@
             pltpu.SemaphoreType.DMA((5,)),
             pltpu.SemaphoreType.DMA,
         ],
-        compiler_params=pltpu.CompilerParams(has_side_effects=True),
+        compiler_params=pltpu.CompilerParams(has_side_effects=True, collective_id=0),
         name="share",
     )(z_t, p_t, tgt)
 
 
 def round_of(t):
-    late = jnp.minimum(t // 2, 1)
-    is_b = (t % 2) * late
-    a = t * (1 - late) + (1 + t // 2) * late
-    is_h = (1 - is_b) * (a // 4)
-    g = is_b * (t // 2 - 1) + (1 - is_b) * (a - 4 * is_h)
+    is_b = t // 3
+    is_h = (t // 2) * (1 - is_b)
+    g = 2 * ((t + is_b) % 2) * (1 - is_h)
     return is_b, is_h, g
 
 
 def gram_kernel(
-    white, pm_ref, out, pm_out,
-    wbuf, pay, y1, y2, zs, zr, xk, xs, xr, fin, fint, own, pmr,
-    g_s, g_r, p_s, p_r, y1_s, y1_r, y2_s, y2_r, z_s, z_r, x_s, x_r, pm_s, pm_r, f_s, own_sem, w_sem,
+    noise, white, pm_ref, proj_ref, tgt, square, cov, prec, nat, out, nat_out, sum_out,
+    wbuf, pay, y1, y2, zs, zr, xk, xs, xr, qay, qx, qs, q1, q2, qz, qr, fin, fint, own, pmr, vec, vy, vz, vx,
+    g_s, g_r, p_s, p_r, y1_s, y1_r, y2_s, y2_r, z_s, z_r, x_s, x_r,
+    qx_s, qx_r, q1_s, q1_r, q2_s, q2_r, qz_s, qz_r, pm_s, pm_r, f_s, own_sem, w_sem, v_s, v_r,
 ):
     z, lo, y, hi, core = place()
     mine = hi * 2 + core
@@ -111,6 +118,29 @@
 
     load = pltpu.make_async_copy(white, wbuf.at[core], w_sem)
     load.start()
+    line = [
+        (z, (lo + d // 4) % 2, y, (hi + (d // 2) % 2) % 2, (core + d % 2) % 2) for d in range(1, 8)
+    ]
+    over_y = [(z, lo, (y + d) % 4, hi, core) for d in range(1, 4)]
+    over_z = [((z + d) % 8, lo, y, hi, core) for d in range(1, 8)]
+    greet(over_y + over_z + line)
+
+    def vec_into(k):
+        return (vy.at[0], vz.at[0], vx.at[pl.ds(0, 1)], vy.at[1], vz.at[1], vx.at[pl.ds(1, 7)])[k]
+
+    def vec_send(k, src):
+        for i, to in enumerate((over_y, over_z, [(z, 1 - lo, y, hi, core)], over_y, over_z, line)[k]):
+            remote(src, vec_into(k).at[i], v_s.at[k], v_r.at[k], to).start()
+
+    def vec_sum(k, src):
+        into = vec_into(k)
+        remote(into, into, v_s.at[k], v_r.at[k], partner).wait_recv()
+        total = src[...]
+        for i in range(into.shape[0]):
+            total = total + into[i]
+        return total
+
+    vec_send(0, proj_ref)
     pm_to = (partner, (z, 1 - lo, y, 1 - hi, core), (z, 1 - lo, y, 1 - hi, 1 - core))
     pm_copies = [remote(pm_ref, pmr.at[k], pm_s.at[k], pm_r.at[k], to) for k, to in enumerate(pm_to)]
     for c in pm_copies:
@@ -133,98 +163,159 @@
         rows = pl.ds(0, 256)
         return remote(wbuf.at[core, rows], wbuf.at[2, rows], g_s.at[g], g_r.at[g], gather_to)
 
+    up_y, down_y = (z, lo, yp, hi, core), (z, lo, ym, hi, core)
+    over_x = (z, 1 - lo, y, hi, core)
+
+    def block(k, size):
+        return pl.ds(pl.multiple_of(k * size, size), size)
+
     def y1_copies(t):
-        up = pl.ds(pl.multiple_of(y2p * 64, 64), 32)
-        down = pl.ds(pl.multiple_of(y2p * 64 + 32, 32), 32)
         return (
-            remote(pay.at[t, up], y1.at[t, 0], y1_s.at[t, 0], y1_r.at[t, 0], (z, lo, yp, hi, core)),
-            remote(pay.at[t, down], y1.at[t, 1], y1_s.at[t, 1], y1_r.at[t, 1], (z, lo, ym, hi, core)),
+            remote(pay.at[t, block(2 * y2p, 32)], y1.at[t, 0], y1_s.at[t, 0], y1_r.at[t, 0], up_y),
+            remote(pay.at[t, block(2 * y2p + 1, 32)], y1.at[t, 1], y1_s.at[t, 1], y1_r.at[t, 1], down_y),
         )
 
     def y2_copies(t):
-        up = pl.ds(pl.multiple_of(yp * 64, 64), 64)
-        down = pl.ds(pl.multiple_of(ym * 64, 64), 64)
         return (
-            remote(pay.at[t, up], y2.at[t, 0], y2_s.at[t, 0], y2_r.at[t, 0], (z, lo, yp, hi, core)),
-            remote(pay.at[t, down], y2.at[t, 1], y2_s.at[t, 1], y2_r.at[t, 1], (z, lo, ym, hi, core)),
+            remote(pay.at[t, block(yp, 64)], y2.at[t, 0], y2_s.at[t, 0], y2_r.at[t, 0], up_y),
+            remote(pay.at[t, block(ym, 64)], y2.at[t, 1], y2_s.at[t, 1], y2_r.at[t, 1], down_y),
         )
 
-    def z_copy(t, d):
-        to = (z + d) % 8
-        cols = pl.ds(pl.multiple_of(to * 128, 128), 128)
-        return remote(zs.at[t, :, cols], zr.at[t, d - 1], z_s.at[t], z_r.at[t], (to, lo, y, hi, core))
+    def z_send(t):
+        for d in range(1, 8):
+            to = (z + d) % 8
+            remote(zs.at[t, :, block(to, 128)], zr.at[t, d - 1], z_s.at[t], z_r.at[t], over_z[d - 1]).start()
 
     def z_all(t):
-        return remote(zr.at[t], zr.at[t], z_s.at[t], z_r.at[t], ((z + 1) % 8, lo, y, hi, core))
+        return remote(zr.at[t], zr.at[t], z_s.at[t], z_r.at[t], over_x)
 
     def x_copy(t):
-        return remote(xs.at[t], xr.at[t], x_s.at[t], x_r.at[t], (z, 1 - lo, y, hi, core))
+        return remote(xs.at[t], xr.at[t], x_s.at[t], x_r.at[t], over_x)
+
+    def qx_copy(t):
+        return remote(qay.at[t, block(1 - lo, 128)], qx.at[t], qx_s.at[t], qx_r.at[t], over_x)
+
+    def q1_copies(t):
+        return (
+            remote(qs.at[t, block(2 * y2p, 16)], q1.at[t, 0], q1_s.at[t, 0], q1_r.at[t, 0], up_y),
+            remote(qs.at[t, block(2 * y2p + 1, 16)], q1.at[t, 1], q1_s.at[t, 1], q1_r.at[t, 1], down_y),
+        )
+
+    def q2_copies(t):
+        return (
+            remote(qs.at[t, block(yp, 32)], q2.at[t, 0], q2_s.at[t, 0], q2_r.at[t, 0], up_y),
+            remote(qs.at[t, block(ym, 32)], q2.at[t, 1], q2_s.at[t, 1], q2_r.at[t, 1], down_y),
+        )
+
+    def qz_send(t):
+        for d in range(1, 8):
+            to = (z + d) % 8
+            remote(qz.at[t, :, block(to, 128)], qr.at[t, d - 1], qz_s.at[t], qz_r.at[t], over_z[d - 1]).start()
+
+    def qz_all(t):
+        return remote(qr.at[t], qr.at[t], qz_s.at[t], qz_r.at[t], over_x)
+
+    def slab(t, g, groups, into):
+        is_b, is_h, _ = round_of(t)
+        plain = 1 - is_h
+        left = is_b * 2 + is_h + plain * (1 - is_b) * core
+        right = plain * core
+        shift = g + is_h * 2 * core
+        a = jnp.concatenate([wbuf[left, pl.ds(pl.multiple_of(k * 128 + 32 * shift, 32), 32), :] for k in groups], axis=0)
+        for j in range(4):
+            b = wbuf[right, j * 256 : (j + 1) * 256, :]
+            part = lax.dot_general(a, b, (((1,), (1,)), ((), ())), preferred_element_type=F32)
+            into[t, :, j * 256 : (j + 1) * 256] = part.astype(BF16)
 
     def compute(t):
         is_b, is_h, g = round_of(t)
-        plain = 1 - is_h
+
+        @pl.when(is_h == 1)
+        def _():
+            to_partner.wait_recv()
+
+        @pl.when(is_b == 1)
+        def _():
+            gather_all(g + 1).wait_recv()
+
+        slab(t, g + 1, (0, 2, 4, 6, 1, 3, 5, 7), qay)
+        qx_copy(t).start()
 
         @pl.when(is_b == 1)
         def _():
             gather_all(g).wait_recv()
 
-        @pl.when(is_h * (1 - g) == 1)
-        def _():
-            to_partner.wait_recv()
-
-        left = is_b * 2 + is_h + plain * (1 - is_b) * core
-        right = plain * core
-        shift = g + is_h * 2 * core
-        a = jnp.concatenate(
-            [wbuf[left, pl.ds(pl.multiple_of(k * 128 + 32 * shift, 32), 32), :] for k in range(8)], axis=0
-        )
-        for j in range(4):
-            b = wbuf[right, j * 256 : (j + 1) * 256, :]
-            part = lax.dot_general(a, b, (((1,), (1,)), ((), ())), preferred_element_type=F32)
-            pay[t, :, j * 256 : (j + 1) * 256] = part.astype(BF16)
+        slab(t, g, range(8), pay)
         for c in y1_copies(t):
             c.start()
 
-    def after_y1(t):
+    def after_1(t):
+        qx_copy(t).wait_recv()
+        qs[t] = (qay[t, block(lo, 128), :].astype(F32) + qx[t].astype(F32)).astype(BF16)
+        for c in q1_copies(t):
+            c.start()
         for k, c in enumerate(y1_copies(t)):
             c.wait_recv()
-            rows = pl.ds(pl.multiple_of((yp, ym)[k] * 64 + 32 * k, 32), 32)
+            rows = block(2 * (yp, ym)[k] + k, 32)
             pay[t, rows, :] = (pay[t, rows, :].astype(F32) + y1[t, k].astype(F32)).astype(BF16)
         for c in y2_copies(t):
             c.start()
 
-    def after_y2(t):
+    def after_2(t):
+        for k, c in enumerate(q1_copies(t)):
+            c.wait_recv()
+            rows = block(2 * (yp, ym)[k] + k, 16)
+            qs[t, rows, :] = (qs[t, rows, :].astype(F32) + q1[t, k].astype(F32)).astype(BF16)
+        for c in q2_copies(t):
+            c.start()
         for c in y2_copies(t):
             c.wait_recv()
-        rows = pl.ds(pl.multiple_of(y * 64, 64), 64)
-        total = pay[t, rows, :].astype(F32) + y2[t, 0].astype(F32) + y2[t, 1].astype(F32)
+        total = pay[t, block(y, 64), :].astype(F32) + y2[t, 0].astype(F32) + y2[t, 1].astype(F32)
         zs[t] = total.astype(BF16)
-        for d in range(1, 8):
-            z_copy(t, d).start()
-
-    def after_z(t):
+        z_send(t)
+
+    def after_3(t):
+        for c in q2_copies(t):
+            c.wait_recv()
+        total = qs[t, block(y, 32), :].astype(F32) + q2[t, 0].astype(F32) + q2[t, 1].astype(F32)
+        qz[t] = total.astype(BF16)
+        qz_send(t)
         z_all(t).wait_recv()
-        total = zs[t, :, pl.ds(pl.multiple_of(z * 128, 128), 128)].astype(F32)
+        total = zs[t, :, block(z, 128)].astype(F32)
         for d in range(7):
             total = total + zr[t, d].astype(F32)
         xk[t] = total
-
-        xs[t] = xk[t, pl.ds(pl.multiple_of((1 - lo) * 32, 32), 32), :].astype(BF16)
+        xs[t] = xk[t, block(1 - lo, 32), :].astype(BF16)
         x_copy(t).start()
 
-    def after_x(t):
+    def after_4(t):
+        is_b, is_h, g = round_of(t)
+        slot = is_b + 2 * is_h
+        row = g + is_h * core * 2
         x_copy(t).wait_recv()
-        is_b, is_h, g = round_of(t)
-        total = xk[t, pl.ds(pl.multiple_of(lo * 32, 32), 32), :] + xr[t].astype(F32)
-        slot = is_b + 2 * is_h
-        row = g * 32 + is_h * core * 64
-        fin[slot, pl.ds(pl.multiple_of(row, 32), 32), :] = total.astype(BF16)
+        total = xk[t, block(lo, 32), :] + xr[t].astype(F32)
+        fin[slot, block(row, 32), :] = total.astype(BF16)
+        qz_all(t).wait_recv()
+        total = qz[t, :, block(z, 128)].astype(F32)
+        for d in range(7):
+            total = total + qr[t, d].astype(F32)
+        fin[slot, block(row + 1, 32), :] = total.astype(BF16)
 
     zero = jnp.zeros((128, 128), BF16)
     fin[2] = zero
 
     def step(t, carry):
-        for lag, work in ((4, after_x), (3, after_z), (2, after_y2), (1, after_y1), (0, compute)):
+        @pl.when(t == 2)
+        def _():
+            vec[0] = vec_sum(0, proj_ref)
+            vec_send(1, vec.at[0])
+
+        @pl.when(t == 4)
+        def _():
+            vec[1] = vec_sum(1, vec.at[0])
+            vec_send(2, vec.at[1])
+
+        for lag, work in ((4, after_4), (3, after_3), (2, after_2), (1, after_1), (0, compute)):
 
             @pl.when((t >= lag) & (t < ROUNDS + lag))
             def _(lag=lag, work=work):
@@ -271,19 +362,40 @@
 
     for c in pm_copies:
         c.wait_recv()
-    pm_out[...] = pm_ref[...] + pmr[0] + pmr[1] + pmr[2]
+    resid = tgt[...] - (pm_ref[...] + pmr[0] + pmr[1] + pmr[2])
+    per_noise = 0.5 / noise[0]
+    nat_out[...] = 0.5 * nat[...] + vec_sum(2, vec.at[1]) * per_noise
 
     pltpu.make_async_copy(own.at[0], own.at[0], own_sem.at[0]).wait()
     both = core * (1 - jnp.minimum(jnp.abs(z // 2 - low), 1))
-
-    @pl.when(both == 0)
-    def _():
-        out[...] = own[0]
 
     @pl.when(both == 1)
     def _():
         pltpu.make_async_copy(own.at[1], own.at[1], own_sem.at[1]).wait()
-        out[...] = own[0] + own[1]
+        own[0] = own[0] + own[1]
+
+    total = 0.25 * resid * resid - square[...]
+    for j in range(8):
+        cols = slice(128 * j, 128 * j + 128)
+        for i in range(8):
+            rows = slice(8 * i, 8 * i + 8)
+            total = total + cov[rows, cols] * own[0, rows, cols].astype(F32)
+    vec[2] = total
+    vec_send(3, vec.at[2])
+    gap = ((z * 2 + lo) * 4 + y) * 64 - mine * 1024
+    for i in range(8):
+        rows = slice(8 * i, 8 * i + 8)
+        shape = (8, 1024)
+        same = lax.broadcasted_iota(jnp.int32, shape, 1) - lax.broadcasted_iota(jnp.int32, shape, 0) == gap + 8 * i
+        out[rows] = 0.5 * prec[rows] + (jnp.where(same, 0.5, 0.0) + own[0, rows].astype(F32) * per_noise)
+    vec[3] = vec_sum(3, vec.at[2])
+    vec_send(4, vec.at[3])
+    vec[4] = vec_sum(4, vec.at[3])
+    vec_send(5, vec.at[4])
+    sum_out[...] = vec_sum(5, vec.at[4])
+    for k in range(6):
+        into = vec_into(k)
+        remote(into, into, v_s.at[k], v_r.at[k], partner).wait_send()
 
     for k, (src, dst, sem, to) in enumerate(sends):
 
@@ -296,24 +408,24 @@
     to_partner.wait_send()
 
     def drain(t, carry):
-        for c in y1_copies(t) + y2_copies(t):
+        for c in y1_copies(t) + y2_copies(t) + q1_copies(t) + q2_copies(t):
             c.wait_send()
-        z_all(t).wait_send()
-        x_copy(t).wait_send()
+        for c in (z_all(t), x_copy(t), qz_all(t), qx_copy(t)):
+            c.wait_send()
         return carry
 
     lax.fori_loop(0, ROUNDS, drain, 0)
     lax.fori_loop(0, 4, lambda g, c: (gather_all(g).wait_send(), c)[1], 0)
 
 
-def gram_reduced(white, pm):
+def gram_reduced(noise, white, pm, proj, tgt, square, cov, prec, nat):
     dma = pltpu.SemaphoreType.DMA
     n = white.shape[1]
     return pl.pallas_call(
         gram_kernel,
-        out_shape=(jax.ShapeDtypeStruct((64, 1024), BF16), jax.ShapeDtypeStruct((8, 128), F32)),
-        in_specs=[ANY, VMEM],
-        out_specs=(VMEM, VMEM),
+        out_shape=tuple(jax.ShapeDtypeStruct(s, F32) for s in ((64, 1024), (8, 128), (8, 128))),
+        in_specs=[pl.BlockSpec(memory_space=pltpu.SMEM), ANY] + [VMEM] * 7,
+        out_specs=(VMEM, VMEM, VMEM),
         scratch_shapes=[
             pltpu.VMEM((3, 1024, n), BF16),
             pltpu.VMEM((ROUNDS, 256, 1024), BF16),
@@ -324,18 +436,31 @@
             pltpu.VMEM((ROUNDS, 64, 128), F32),
             pltpu.VMEM((ROUNDS, 32, 128), BF16),
             pltpu.VMEM((ROUNDS, 32, 128), BF16),
+            pltpu.VMEM((ROUNDS, 256, 1024), BF16),
+            pltpu.VMEM((ROUNDS, 128, 1024), BF16),
+            pltpu.VMEM((ROUNDS, 128, 1024), BF16),
+            pltpu.VMEM((ROUNDS, 2, 16, 1024), BF16),
+            pltpu.VMEM((ROUNDS, 2, 32, 1024), BF16),
+            pltpu.VMEM((ROUNDS, 32, 1024), BF16),
+            pltpu.VMEM((ROUNDS, 7, 32, 128), BF16),
             pltpu.VMEM((3, 128, 128), BF16),
             pltpu.VMEM((2, 128, 128), BF16),
             pltpu.VMEM((2, 64, 1024), BF16),
             pltpu.VMEM((3, 8, 128), F32),
+            pltpu.VMEM((5, 8, 128), F32),
+            pltpu.VMEM((2, 3, 8, 128), F32),
+            pltpu.VMEM((2, 7, 8, 128), F32),
+            pltpu.VMEM((8, 8, 128), F32),
             dma((4,)), dma((4,)), dma, dma,
             dma((ROUNDS, 2)), dma((ROUNDS, 2)), dma((ROUNDS, 2)), dma((ROUNDS, 2)),
             dma((ROUNDS,)), dma((ROUNDS,)), dma((ROUNDS,)), dma((ROUNDS,)),
-            dma((3,)), dma((3,)), dma((9,)), dma((2,)), dma,
+            dma((ROUNDS,)), dma((ROUNDS,)), dma((ROUNDS, 2)), dma((ROUNDS, 2)),
+            dma((ROUNDS, 2)), dma((ROUNDS, 2)), dma((ROUNDS,)), dma((ROUNDS,)),
+            dma((3,)), dma((3,)), dma((9,)), dma((2,)), dma, dma((6,)), dma((6,)),
         ],
-        compiler_params=pltpu.CompilerParams(has_side_effects=True, vmem_limit_bytes=40 * 2**20),
+        compiler_params=pltpu.CompilerParams(has_side_effects=True, collective_id=1, vmem_limit_bytes=40 * 2**20),
         name="gram_reduced",
-    )(white, pm)
+    )(noise, white, pm, proj, tgt, square, cov, prec, nat)
 
 
 def three_parts(v):
@@ -363,22 +488,22 @@
     pm = jnp.sum(mean_v[:, None] * wide, axis=0)
     proj = jnp.sum(wide * tgt_row[None, :], axis=1)
     square = jnp.sum(wide * wide)
-    gram_t, pm = gram_reduced(white, jnp.pad(pm, (0, 1024 - own_points)).reshape(8, 128))
-    gram_t = gram_t.astype(F32)
-    trace = jnp.sum(covariance.T * gram_t)
-    fit = 0.25 * (jnp.sum(jnp.square(tgt - pm)) + signal * own_points) - square
-    mine = lax.axis_index(IND)
-    slots = jnp.where(jnp.arange(4)[:, None] == mine, proj[None, :], 0.0).reshape(-1)
-    total = lax.psum(jnp.concatenate([slots, (trace + fit)[None]]), AXES)
-    proj = lax.dynamic_slice(total, (mine * own_rows,), (own_rows,))
+    precision_new, natural_new, total = gram_reduced(
+        noise_var[None],
+        white,
+        jnp.pad(pm, (0, 1024 - own_points)).reshape(8, 128),
+        proj.reshape(8, 128),
+        tgt,
+        jnp.full((8, 128), square / 1024, F32),
+        covariance.T,
+        precision.T,
+        natural_one.reshape(8, 128),
+    )
     count = own_points * lax.axis_size(DP_REP)
-    expected_fit = -0.5 * jnp.log(2.0 * jnp.pi * noise_var) - total[-1] / (2.0 * noise_var * count)
-    row_ids = mine * own_rows + jnp.arange(own_rows, dtype=jnp.int32)
-    col_ids = lax.axis_index(DP_REP) * 64 + jnp.arange(64, dtype=jnp.int32)
-    identity = (row_ids[None, :] == col_ids[:, None]).astype(F32)
-    precision_new = (0.5 * precision.T + 0.5 * (identity + gram_t / noise_var)).T
-    natural_new = 0.5 * natural_one + 0.5 * proj / noise_var
-    return precision_new, natural_new, expected_fit
+    expected_fit = -0.5 * jnp.log(2.0 * jnp.pi * noise_var) - (jnp.sum(total) + signal * count) / (
+        2.0 * noise_var * count
+    )
+    return precision_new.T, natural_new.reshape(own_rows), expected_fit
 
 
 def solution(mesh):

time: 232 us -> 132 us (0.57)
  blocking collectives: 75.8 us -> 0 us
  Pallas kernels: 125 us -> 105 us
  other arithmetic: 10.9 us -> 7.34 us
    psum x1 -> x0, blocking collectives: 75.8 us -> none  [shards(): total = lax.psum(jnp.concatenate([slots, (trace + fit)[None]]), AXES)]
    pallas_call x1, Pallas kernels: 26.8 us -> 14.4 us  [share(): pl.pallas_call(share_kernel, out_shape=(jax.ShapeDtypeStruct((4, *z_t.sha...]
    pallas_call x1, Pallas kernels: 98.1 us -> 90.3 us  [gram_reduced(): pl.pallas_call(gram_kernel, out_shape=tuple((jax.ShapeDtypeStruct(s, F32)...]
where the time goes in v2:
time: 132 us; the launch traced here: 131 us
  Pallas kernels  105 us (80%)
  matrix products  10.7 us (8%)
  other arithmetic  7.34 us (6%)
  between operations  5.31 us (4%)
  local copies, waits for them, and re-layouts  3.23 us (2%)
    pallas_call x1, Pallas kernels, gram_reduced(): pl.pallas_call(gram_kernel, out_shape=tuple((jax.ShapeDtypeStruct(s, F32)...  90.3 us
    pallas_call x1, Pallas kernels, share(): pl.pallas_call(share_kernel, out_shape=(jax.ShapeDtypeStruct((4, *z_t.sha...  14.4 us
    dot_general x1, matrix products, shards(): white = jnp.dot(whitening, cross, preferred_element_type=F32).astype(BF16)  7.7 us
    convert_element_type x1, other arithmetic, shards(): (signal * jnp.exp(-0.5 * (norm_z[:, None] + norm_x[None, :] - 2.0 * inner...  4.18 us
    dot_general x1, matrix products, shards(): lax.dot_general(parts, jnp.concatenate([pts] * 3, axis=0), (((1,), (0,)),...  3.01 us

profile of v2, /device:TPU:1, one launch (start us, length us, event | category | flops | bytes accessed | tf_op | source)
XLA Modules:
  0.0 131.3 jit_solution(9064641493811517944)
XLA Ops:
  0.6 1.3 pad_bitcast_fusion.1.t_ref
  1.9 14.4 %share.1 = (f32[4,64,1024]{2,1,0:T(8,128)}, bf16[64,768]{1,0:T(8,128)(2,1)}, f32[8,128]{1,0:T(8,128)}) custom-call(f32[64,1024]{1,0:T(8,128)} %bitcast.44, bf16[64,768]{1,0:T(8,128)(2,1)} %bitcast.45, f32[8,128]{1,0:T(8,128)} %pad_bitcast_fusion.1.t_ref), custom_call_target="tpu_custom_call" | custom-call | tf_op jit(solution)/shard_map/share/pallas_call | solution.py:81
  16.3 0.7 mul.63
  17.0 1.7 %reduce-precision_convert_fusion.1 = (bf16[4,64,1024]{2,1,0:T(8,128)(2,1)S(1)}, bf16[4,64,1024]{2,1,0:T(8,128)(2,1)S(1)}, bf16[4,64,1024]{2,1,0:T(8,128)(2,1)S(1)}, f32[4,1024]{1,0:T(4,128)S(1)}) fusion(f32[4,64,1024]{2,1,0:T(8,128)} %get-tuple-element.9, f32[64]{0:T(128)S(1)} %mul.63, f32[64]{0:T(128)} %param.18), kind=kLoop, calls=%fused_computation.21 | loop fusion | flops 2879488 | bytes 2638336 | tf_op jit(solution)/shard_map/convert_element_type | solution.py:469
  18.8 0.0 copy-start.4
  18.8 0.0 copy-start.5
  18.8 0.0 copy-start.6
  18.8 0.0 slice-start
  18.8 3.0 %broadcast_multiply_fusion = f32[4,1024,768]{2,1,0:T(8,128)S(1)} fusion(bf16[4,64,1024]{2,1,0:T(8,128)(2,1)S(1)} %get-tuple-element.20, bf16[4,64,1024]{2,1,0:T(8,128)(2,1)S(1)} %get-tuple-element.19, bf16[4,64,1024]{2,1,0:T(8,128)(2,1)S(1)} %get-tuple-element.18, bf16[64,768]{1,0:T(8,128)(2,1)} %get-tuple-element.10), kind=kOutput, calls=%fused_computation.5 | convolution fusion | flops 1216708608 | bytes 14254080 | tf_op jit(solution)/shard_map/dot_general | solution.py:482
  21.8 0.0 copy-done.4
  21.8 0.0 copy-done.5
  21.9 0.1 multiply_reduce_fusion.1
  22.0 0.0 copy-done.6
  22.0 0.6 fusion.19
  22.6 4.2 %fusion.3 = bf16[4096,768]{1,0:T(8,128)(2,1)S(1)} fusion(f32[4,1024,768]{2,1,0:T(8,128)S(1)} %broadcast_multiply_fusion, f32[768]{0:T(1024)S(1)} %multiply_reduce_fusion.1, f32[4096]{0:T(1024)S(1)} %bitcast.47, f32[]{:T(128)} %bitcast), kind=kLoop, calls=%fused_computation.4 | loop fusion | flops 15728640 | bytes 18893828 | tf_op jit(solution)/shard_map/convert_element_type | solution.py:485
  26.8 0.0 copy-done.2
  26.8 0.0 copy-start
  26.8 0.0 copy-start.1
  26.8 0.0 copy-start.3
  26.9 7.7 %fusion.6 = (f32[]{:T(128)}, f32[1024]{0:T(1024)S(1)}, f32[768]{0:T(1024)S(1)}, bf16[1024,768]{1,0:T(8,128)(2,1)S(1)}) fusion(f32[768]{0:T(1024)S(1)} %slice_bitcast_fusion, f32[1024]{0:T(1024)S(1)} %copy-done.7, bf16[1024,4096]{1,0:T(8,128)(2,1)S(1)} %bitcast.49, bf16[4096,768]{1,0:T(8,128)(2,1)S(1)} %fusion.3), kind=kOutput, calls=%fused_computation.11 | convolution fusion | flops 6448740352 | bytes 16267268 | tf_op jit(solution)/shard_map/dot_general | solution.py:486
  35.3 90.3 %gram_reduced.1 = (f32[64,1024]{1,0:T(8,128)S(1)}, f32[8,128]{1,0:T(8,128)S(1)}, f32[8,128]{1,0:T(8,128)S(1)}) custom-call(f32[1]{0:T(128)} %get-tuple-element.23.noise, bf16[1024,768]{1,0:T(8,128)(2,1)S(1)} %get-tuple-element.24.white, f32[8,128]{1,0:T(8,128)S(1)} %pad_bitcast_fusion.pm_ref, f32[8,128]{1,0:T(8,128)S(1)} %bitcast.42, ...), custom_call_target="tpu_custom_call" | custom-call | tf_op jit(solution)/shard_map/gram_reduced/pallas_call | solution.py:424
  125.6 0.6 reduce_sum.59
  128.9 0.7 copy.20
  129.6 0.6 copy.21
  (14 shorter events, 0.0 us)
Async XLA Ops:
  18.8 3.1 %copy-start.4 = (bf16[64,768]{1,0:T(8,128)(2,1)S(1)}, bf16[64,768]{1,0:T(8,128)(2,1)}, u32[]{:S(2)}) copy-start(bf16[64,768]{1,0:T(8,128)(2,1)} %get-tuple-element.10) | copy-start | bytes 294916
  18.8 3.1 %copy-start.5 = (f32[64]{0:T(128)S(1)}, f32[64]{0:T(128)}, u32[]{:S(2)}) copy-start(f32[64]{0:T(128)} %param.18) | copy-start | bytes 772
  18.8 3.2 %copy-start.6 = (f32[2]{0:T(128)S(1)}, f32[2]{0:T(128)}, u32[]{:S(2)}) copy-start(f32[2]{0:T(128)} %param.19) | copy-start | bytes 28
  18.8 8.0 %slice-start = ((s8[8388608]{0:T(1024)(128)(4,1)}), s8[4194304]{0:T(1024)(128)(4,1)S(1)}, s32[]{:S(2)}) async-start(s8[8388608]{0:T(1024)(128)(4,1)} %bitcast.48), calls=%async_computation | async-start | bytes 8388608
  22.6 4.2 %copy-start.2 = (f32[8,128]{1,0:T(8,128)S(1)}, f32[8,128]{1,0:T(8,128)}, u32[]{:S(2)}) copy-start(f32[8,128]{1,0:T(8,128)} %get-tuple-element.11.tgt) | copy-start | bytes 12292
  22.6 4.2 %slice-start.1 = ((s8[8388608]{0:T(1024)(128)(4,1)}), s8[4194304]{0:T(1024)(128)(4,1)S(1)}, s32[]{:S(2)}) async-start(s8[8388608]{0:T(1024)(128)(4,1)} %bitcast.48), calls=%async_computation.1 | async-start | bytes 8388608
  22.6 4.2 %copy-start.7 = (f32[1024]{0:T(1024)S(1)}, f32[1024]{0:T(1024)}, u32[]{:S(2)}) copy-start(f32[1024]{0:T(1024)} %param.14) | copy-start | bytes 12292
  26.8 8.4 %copy-start = (f32[1024,64]{0,1:T(8,128)S(1)}, f32[1024,64]{0,1:T(8,128)}, u32[]{:S(2)}) copy-start(f32[1024,64]{0,1:T(8,128)} %param.15) | copy-start | bytes 786436
  26.8 8.4 %copy-start.1 = (f32[1024,64]{0,1:T(8,128)S(1)}, f32[1024,64]{0,1:T(8,128)}, u32[]{:S(2)}) copy-start(f32[1024,64]{0,1:T(8,128)} %param.16) | copy-start | bytes 786436
  26.8 8.4 %copy-start.3 = (f32[1024]{0:T(1024)S(1)}, f32[1024]{0:T(1024)}, u32[]{:S(2)}) copy-start(f32[1024]{0:T(1024)} %param.17) | copy-start | bytes 12292

commit v3 on v2

v3 whole, which is shorter than its diff:
```python
import jax
import jax.numpy as jnp
from jax import lax
from jax.experimental import pallas as pl
from jax.experimental.pallas import tpu as pltpu
from jax.sharding import Mesh
from jax.sharding import PartitionSpec as P

AXES = ("dp_0", "dp_1", "rep", "ind_0", "ind_1")
IND = ("ind_0", "ind_1")
DP_REP = ("dp_0", "dp_1", "rep")
MESH = pl.DeviceIdType.MESH
VMEM = pl.BlockSpec(memory_space=pltpu.VMEM)
ANY = pl.BlockSpec(memory_space=pl.ANY)
F32 = jnp.float32
BF16 = jnp.bfloat16
ROUNDS = 5


def place():
    return tuple(lax.axis_index(a) for a in AXES)


def remote(src, dst, send, recv, to):
    return pltpu.make_async_remote_copy(
        src_ref=src, dst_ref=dst, send_sem=send, recv_sem=recv, device_id=to, device_id_type=MESH
    )


def parts_of(v):
    a = v.astype(BF16)
    b = (v - a.astype(F32)).astype(BF16)
    return a, b, (v - a.astype(F32) - b.astype(F32)).astype(BF16)


def tile_of(v):
    row = lax.broadcasted_iota(jnp.int32, (16, v.shape[1]), 0)
    tile = jnp.zeros((16, v.shape[1]), F32)
    for k, part in enumerate(parts_of(v)):
        tile = jnp.where(row == k, part.astype(F32), tile)
    return tile.astype(BF16)


def dot(a, b, dims):
    return lax.dot_general(a, b, ((dims[:1], dims[1:]), ((), ())), preferred_element_type=F32)


def round_of(t):
    is_b = t // 3
    is_h = (t // 2) * (1 - is_b)
    g = 2 * ((t + is_b) % 2) * (1 - is_h)
    return is_b, is_h, g


def kernel(
    hypers, ind_t, pts_in, tgt_in, scale_in, mean, whitening, cov, prec, nat, out, nat_out, fit_out,
    zall, pts, tgt, wv, cross, acc, square, pmv, covb,
    wbuf, pay, y1, y2, zs, zr, xk, xs, xr, qay, qx, qs, q1, q2, qz, qr, fin, fint, own, pmr, vec, vy, vz, vx, va, vb,
    i_s, i_r, c_s, cov_s, cov_r,
    g_s, g_r, p_s, p_r, y1_s, y1_r, y2_s, y2_r, z_s, z_r, x_s, x_r,
    qx_s, qx_r, q1_s, q1_r, q2_s, q2_r, qz_s, qz_r, pm_s, pm_r, f_s, own_sem, v_s, v_r,
):
    z, lo, y, hi, core = place()
    mine = hi * 2 + core
    yp, ym, y2p = (y + 1) % 4, (y + 3) % 4, (y + 2) % 4
    partner = (z, lo, y, hi, 1 - core)
    gather_to = (z, 1 - lo, y, 1 - hi, (core + 1 - hi) % 2)

    count = pts.shape[1]
    cut = wv.shape[2]
    w_copies = [
        pltpu.make_async_copy(
            whitening.at[:, pl.ds(pl.multiple_of((hi + h - 2 * hi * h) * cut, cut), cut)], wv.at[h], c_s.at[h]
        )
        for h in range(2)
    ]
    for c in w_copies:
        c.start()
    line = [
        (z, (lo + d // 4) % 2, y, (hi + (d // 2) % 2) % 2, (core + d % 2) % 2) for d in range(1, 8)
    ]
    over_y = [(z, lo, (y + d) % 4, hi, core) for d in range(1, 4)]
    over_z = [((z + d) % 8, lo, y, hi, core) for d in range(1, 8)]
    low, high = hi * 2, hi * 2 + 1
    nxt = (1 - hi) * 2 + (core + hi) % 2
    prv = (1 - hi) * 2 + (core + 1 - hi) % 2

    def owner(q, ind):
        return (q // 8, (q // 4) % 2, q % 4, ind // 2, ind % 2)

    def flat(d):
        return (((d[0] * 2 + d[1]) * 4 + d[2]) * 2 + d[3]) * 2 + d[4]

    def equal(a, b):
        return 1 - jnp.minimum(jnp.abs(a - b), 1)

    me = flat(place())
    here = 4 * y + 2 * lo
    holders = (
        [owner(16 * mine + here + e, mine) for e in range(2)]
        + [owner(16 * nxt + here + e, mine) for e in range(2)]
        + [owner(16 * mine + 2 * z + e, nxt) for e in range(2)]
        + [owner(16 * high + here + core, low)]
        + [owner(16 * low + 2 * z + e, high) for e in range(2)]
    )
    own_group, own_q = z // 2, (z % 2) * 8 + lo * 4 + y
    is_d, is_n, is_p = equal(own_group, mine), equal(own_group, nxt), equal(own_group, prv)
    is_s = 1 - is_d - is_n - is_p
    mirrored = is_p + is_s * core
    both = is_s * core

    def cov_target(i, second):
        e = own_q % 2
        to_core = is_p * (own_group % 2) + is_s * ((1 - core) * e + core * second) + (1 - is_p - is_s) * core
        to = (
            (1 - mirrored) * i + mirrored * (own_q // 2),
            (1 - mirrored) * ((own_q // 2) % 2) + mirrored * (i % 2),
            (1 - mirrored) * (own_q // 4) + mirrored * (i // 2),
            is_p * (own_group // 2) + (1 - is_p) * hi,
            to_core,
        )
        slot = is_d * e + is_n * (2 + e) + is_p * (4 + e) + is_s * ((1 - core) * 6 + core * (7 + e))
        return to, cov.at[:, pl.ds(pl.multiple_of(i * 128, 128), 128)], covb.at[slot]

    barrier = pltpu.get_barrier_semaphore()
    arrivals = 17 + 8 * (1 + both)
    for to in over_y + over_z + line:
        pl.semaphore_signal(barrier, inc=1, device_id=to, device_id_type=MESH)
    for to in holders:
        arrivals = arrivals - equal(flat(to), me)

        @pl.when(flat(to) != me)
        def _(to=to):
            pl.semaphore_signal(barrier, inc=1, device_id=to, device_id_type=MESH)

    pl.semaphore_wait(barrier, arrivals)

    over_a = [((z + d) % 8, lo, y, hi, (core + c) % 2) for d in range(8) for c in range(2) if d + c]
    over_b = [
        (z, (lo + a) % 2, (y + d) % 4, (hi + b) % 2, core)
        for d in range(4)
        for a in range(2)
        for b in range(2)
        if d + a + b
    ]

    def cov_sends(second, act):
        def one(i, carry):
            to, src, dst = cov_target(i, second)

            @pl.when(flat(to) != me)
            def _():
                act(remote(src, dst, cov_s.at[8 * second + i], cov_r, to), True)

            @pl.when(flat(to) == me)
            def _():
                act(pltpu.make_async_copy(src, dst, cov_r), False)

            return carry

        lax.fori_loop(0, 8, one, 0)

    def cov_start(copy, far):
        copy.start()

    def cov_sent(copy, far):
        if far:
            copy.wait_send()

    def vec_into(k):
        return (vy, vz, vx, va, vb)[k]

    def vec_send(k, src):
        for i, to in enumerate((over_y, over_z, [(z, 1 - lo, y, hi, core)], over_a, over_b)[k]):
            remote(src, vec_into(k).at[i], v_s.at[k], v_r.at[k], to).start()

    def vec_sum(k, src):
        into = vec_into(k)
        remote(into, into, v_s.at[k], v_r.at[k], partner).wait_recv()
        total = src[...]
        return total + sum(into[i] for i in range(into.shape[0]))

    other = (1 - hi) * 2 + core
    across = (z, 1 - lo, y, 1 - hi, core)
    swap = (z, 1 - lo, y, hi, core)
    over = remote(ind_t, zall.at[mine], i_s.at[0], i_r.at[0], across)
    near = remote(ind_t, zall.at[mine], i_s.at[1], i_r.at[1], partner)
    on = remote(zall.at[other], zall.at[other], i_s.at[2], i_r.at[2], partner)
    swaps = (
        remote(pts_in, pts, i_s.at[3], i_r.at[3], swap),
        remote(tgt_in, tgt, i_s.at[4], i_r.at[4], swap),
    )

    @pl.when(hi == 0)
    def _():
        for c in swaps:
            c.start()

    over.start()
    near.start()
    own_z = pltpu.make_async_copy(ind_t, zall.at[mine], c_s.at[2])
    own_z.start()
    cov_sends(0, cov_start)

    @pl.when(both == 1)
    def _():
        cov_sends(1, cov_start)

    @pl.when(hi == 1)
    def _():
        pts[...] = pts_in[...]
        tgt[...] = tgt_in[...]

    own_z.wait()

    @pl.when(hi == 0)
    def _():
        for c in swaps:
            c.wait()

    diagonal = lax.broadcasted_iota(jnp.int32, (64, 64), 0) == lax.broadcasted_iota(jnp.int32, (64, 64), 1)
    scale = jnp.sum(jnp.where(diagonal, jnp.broadcast_to(scale_in[...], (64, 64)), 0.0), axis=1, keepdims=True)
    scales = jnp.broadcast_to(scale, (64, count))
    t_row = jnp.concatenate([tgt[j : j + 1, :] for j in range(count // 128)], axis=1)
    norm_x = 0.5 * jnp.sum(jnp.square(pts[...].astype(F32) / scales), axis=0, keepdims=True)
    three = lax.broadcasted_iota(jnp.int32, (16, count), 0) < 3
    p_mat = jnp.concatenate([pts[...]] * 3 + [jnp.where(three, 1.0, 0.0).astype(BF16)], axis=0)

    def cross_rows(held, half, at):
        def piece(j, carry):
            cols = pl.ds(pl.multiple_of(j * 256, 256), 256)
            zt = zall[held, :, cols]
            s = jnp.broadcast_to(scale, (64, 256))
            zs_ = zt / s
            norm = tile_of(-0.5 * jnp.sum(zs_ * zs_, axis=0, keepdims=True))
            z_mat = jnp.concatenate([*parts_of(zs_ / s), norm], axis=0)
            power = dot(z_mat, p_mat, (0, 0)) - norm_x
            rows = pl.ds(pl.multiple_of(at * 1024 + j * 256, 256), 256)
            cross[half, rows, :] = (hypers[0] * jnp.exp(power)).astype(BF16)
            return carry

        lax.fori_loop(0, 4, piece, 0)

    cross_rows(mine, 0, core)
    near.wait_recv()
    cross_rows(hi * 2 + 1 - core, 0, 1 - core)
    w_copies[0].wait()

    def first_half(i, carry):
        rows = pl.ds(pl.multiple_of(i * 256, 256), 256)
        for j in range(count // 256):
            cols = slice(256 * j, 256 * j + 256)
            acc[rows, cols] = dot(wv[0, rows, :], cross[0, :, cols], (1, 0))
        return carry

    over.wait_recv()
    on.start()
    lax.fori_loop(0, 4, first_half, 0)
    cross_rows(other, 1, core)
    on.wait_recv()
    cross_rows((1 - hi) * 2 + 1 - core, 1, 1 - core)
    w_copies[1].wait()
    square[...] = jnp.zeros((8, 128), F32)

    def gather_piece(g, k):
        rows = pl.ds(pl.multiple_of(k * 128 + 32 * g, 32), 32)
        return remote(wbuf.at[core, rows], wbuf.at[2, rows], g_s.at[g], g_r.at[g], gather_to)

    def second_half(g, carry):
        rows = [pl.ds(pl.multiple_of(k * 128 + 32 * g, 32), 32) for k in range(8)]
        a = jnp.concatenate([wv[1, r, :] for r in rows], axis=0)
        for j in range(count // 256):
            cols = slice(256 * j, 256 * j + 256)
            part = dot(a, cross[1, :, cols], (1, 0)) + jnp.concatenate([acc[r, cols] for r in rows], axis=0)
            part = part.astype(BF16)
            for k, r in enumerate(rows):
                wbuf[core, r, cols] = part[32 * k : 32 * k + 32]
            wide = part.astype(F32)
            both = jnp.sum((wide * wide).reshape(32, 8, 256), axis=0)
            square[...] += both[:, :128] + both[:, 128:]
        lax.fori_loop(0, 8, lambda k, c: (gather_piece(g, k).start(), c)[1], 0)
        return carry

    lax.fori_loop(0, 4, second_half, 0)
    to_partner = remote(wbuf.at[core], wbuf.at[core], p_s, p_r, partner)
    to_partner.start()
    m_row = jnp.concatenate([mean[j : j + 1, :] for j in range(8)], axis=1)
    pmv[...] = jnp.sum(dot(tile_of(m_row), wbuf[core], (1, 0)), axis=0, keepdims=True)
    pm_to = (partner, (z, 1 - lo, y, 1 - hi, core), (z, 1 - lo, y, 1 - hi, 1 - core))
    pm_copies = [remote(pmv, pmr.at[k], pm_s.at[k], pm_r.at[k], to) for k, to in enumerate(pm_to)]
    for c in pm_copies:
        c.start()
    proj = jnp.sum(dot(tile_of(t_row), wbuf[core], (1, 1)), axis=0, keepdims=True)
    vec[2] = jnp.concatenate([proj[:, 128 * j : 128 * j + 128] for j in range(8)], axis=0)
    vec_send(0, vec.at[2])

    def gather_all(g):
        rows = pl.ds(0, 256)
        return remote(wbuf.at[core, rows], wbuf.at[2, rows], g_s.at[g], g_r.at[g], gather_to)

    up_y, down_y = (z, lo, yp, hi, core), (z, lo, ym, hi, core)
    over_x = (z, 1 - lo, y, hi, core)

    def block(k, size):
        return pl.ds(pl.multiple_of(k * size, size), size)

    def y1_copies(t):
        return (
            remote(pay.at[t, block(2 * y2p, 32)], y1.at[t, 0], y1_s.at[t, 0], y1_r.at[t, 0], up_y),
            remote(pay.at[t, block(2 * y2p + 1, 32)], y1.at[t, 1], y1_s.at[t, 1], y1_r.at[t, 1], down_y),
        )

    def y2_copies(t):
        return (
            remote(pay.at[t, block(yp, 64)], y2.at[t, 0], y2_s.at[t, 0], y2_r.at[t, 0], up_y),
            remote(pay.at[t, block(ym, 64)], y2.at[t, 1], y2_s.at[t, 1], y2_r.at[t, 1], down_y),
        )

    def z_send(t):
        for d in range(1, 8):
            to = (z + d) % 8
            remote(zs.at[t, :, block(to, 128)], zr.at[t, d - 1], z_s.at[t], z_r.at[t], over_z[d - 1]).start()

    def z_all(t):
        return remote(zr.at[t], zr.at[t], z_s.at[t], z_r.at[t], over_x)

    def x_copy(t):
        return remote(xs.at[t], xr.at[t], x_s.at[t], x_r.at[t], over_x)

    def qx_copy(t):
        return remote(qay.at[t, block(1 - lo, 128)], qx.at[t], qx_s.at[t], qx_r.at[t], over_x)

    def q1_copies(t):
        return (
            remote(qs.at[t, block(2 * y2p, 16)], q1.at[t, 0], q1_s.at[t, 0], q1_r.at[t, 0], up_y),
            remote(qs.at[t, block(2 * y2p + 1, 16)], q1.at[t, 1], q1_s.at[t, 1], q1_r.at[t, 1], down_y),
        )

    def q2_copies(t):
        return (
            remote(qs.at[t, block(yp, 32)], q2.at[t, 0], q2_s.at[t, 0], q2_r.at[t, 0], up_y),
            remote(qs.at[t, block(ym, 32)], q2.at[t, 1], q2_s.at[t, 1], q2_r.at[t, 1], down_y),
        )

    def qz_send(t):
        for d in range(1, 8):
            to = (z + d) % 8
            remote(qz.at[t, :, block(to, 128)], qr.at[t, d - 1], qz_s.at[t], qz_r.at[t], over_z[d - 1]).start()

    def qz_all(t):
        return remote(qr.at[t], qr.at[t], qz_s.at[t], qz_r.at[t], over_x)

    def slab(t, g, groups, into):
        is_b, is_h, _ = round_of(t)
        plain = 1 - is_h
        left = is_b * 2 + is_h + plain * (1 - is_b) * core
        right = plain * core
        shift = g + is_h * 2 * core
        a = jnp.concatenate([wbuf[left, pl.ds(pl.multiple_of(k * 128 + 32 * shift, 32), 32), :] for k in groups], axis=0)
        for j in range(4):
            b = wbuf[right, j * 256 : (j + 1) * 256, :]
            part = dot(a, b, (1, 1))
            into[t, :, j * 256 : (j + 1) * 256] = part.astype(BF16)

    def compute(t):
        is_b, is_h, g = round_of(t)

        @pl.when(is_h == 1)
        def _():
            to_partner.wait_recv()

        @pl.when(is_b == 1)
        def _():
            gather_all(g + 1).wait_recv()

        slab(t, g + 1, (0, 2, 4, 6, 1, 3, 5, 7), qay)
        qx_copy(t).start()

        @pl.when(is_b == 1)
        def _():
            gather_all(g).wait_recv()

        slab(t, g, range(8), pay)
        for c in y1_copies(t):
            c.start()

    def after_1(t):
        qx_copy(t).wait_recv()
        qs[t] = (qay[t, block(lo, 128), :].astype(F32) + qx[t].astype(F32)).astype(BF16)
        for c in q1_copies(t):
            c.start()
        for k, c in enumerate(y1_copies(t)):
            c.wait_recv()
            rows = block(2 * (yp, ym)[k] + k, 32)
            pay[t, rows, :] = (pay[t, rows, :].astype(F32) + y1[t, k].astype(F32)).astype(BF16)
        for c in y2_copies(t):
            c.start()

    def after_2(t):
        for k, c in enumerate(q1_copies(t)):
            c.wait_recv()
            rows = block(2 * (yp, ym)[k] + k, 16)
            qs[t, rows, :] = (qs[t, rows, :].astype(F32) + q1[t, k].astype(F32)).astype(BF16)
        for c in q2_copies(t):
            c.start()
        for c in y2_copies(t):
            c.wait_recv()
        total = pay[t, block(y, 64), :].astype(F32) + y2[t, 0].astype(F32) + y2[t, 1].astype(F32)
        zs[t] = total.astype(BF16)
        z_send(t)

    def after_3(t):
        for c in q2_copies(t):
            c.wait_recv()
        total = qs[t, block(y, 32), :].astype(F32) + q2[t, 0].astype(F32) + q2[t, 1].astype(F32)
        qz[t] = total.astype(BF16)
        qz_send(t)
        z_all(t).wait_recv()
        total = zs[t, :, block(z, 128)].astype(F32)
        for d in range(7):
            total = total + zr[t, d].astype(F32)
        xk[t] = total
        xs[t] = xk[t, block(1 - lo, 32), :].astype(BF16)
        x_copy(t).start()

    def after_4(t):
        is_b, is_h, g = round_of(t)
        slot = is_b + 2 * is_h
        row = g + is_h * core * 2
        x_copy(t).wait_recv()
        total = xk[t, block(lo, 32), :] + xr[t].astype(F32)
        fin[slot, block(row, 32), :] = total.astype(BF16)
        qz_all(t).wait_recv()
        total = qz[t, :, block(z, 128)].astype(F32)
        for d in range(7):
            total = total + qr[t, d].astype(F32)
        fin[slot, block(row + 1, 32), :] = total.astype(BF16)

    zero = jnp.zeros((128, 128), BF16)
    fin[2] = zero

    def step(t, carry):
        @pl.when(t == 3)
        def _():
            vec[0] = vec_sum(0, vec.at[2])
            vec_send(1, vec.at[0])

        @pl.when(t == 6)
        def _():
            vec[1] = vec_sum(1, vec.at[0])
            vec_send(2, vec.at[1])

        for lag, work in ((8, after_4), (6, after_3), (4, after_2), (2, after_1), (0, compute)):

            @pl.when((t >= lag) & (t < ROUNDS + lag))
            def _(lag=lag, work=work):
                work(t - lag)

        return carry

    lax.fori_loop(0, ROUNDS + 8, step, 0)

    fint[0] = fin[1].astype(F32).T.astype(BF16)
    fint[1] = fin[2].astype(F32).T.astype(BF16)

    direct = block(z, 128)
    mirror = block(2 * y + lo, 128)
    half = block(core, 64)
    pieces = [fin.at[0, pl.ds(64 * e, 64)] for e in range(2)] + [fin.at[1, pl.ds(64 * e, 64)] for e in range(2)]
    pieces += [fint.at[0, pl.ds(64 * e, 64)] for e in range(2)]
    pieces += [fin.at[2, half]] + [fint.at[1, pl.ds(64 * e, 64)] for e in range(2)]
    places = [own.at[0, :, direct]] * 4 + [own.at[0, :, mirror]] * 2 + [own.at[0, :, direct]] + [own.at[core, :, mirror]] * 2
    sems = [own_sem.at[0]] * 7 + [own_sem.at[core]] * 2
    sends = list(zip(pieces, places, sems, holders))

    for k, (src, dst, sem, to) in enumerate(sends):

        @pl.when(flat(to) != me)
        def _(k=k, src=src, dst=dst, sem=sem, to=to):
            remote(src, dst, f_s.at[k], sem, to).start()

        @pl.when(flat(to) == me)
        def _(src=src, dst=dst, sem=sem):
            pltpu.make_async_copy(src, dst, sem).start()

    for c in pm_copies:
        c.wait_recv()
    resid = t_row - (pmv[...] + pmr[0] + pmr[1] + pmr[2])
    resid = resid * resid
    total = sum(resid[:, 128 * j : 128 * j + 128] for j in range(count // 128))
    total = jnp.broadcast_to(total / 32, (8, 128)) - square[...]
    pltpu.make_async_copy(covb, covb, cov_r).wait()
    for k, piece in enumerate(pieces):
        total = total + jnp.sum((covb[k] * piece[...].astype(F32)).reshape(8, 8, 128), axis=0)
    vec[3] = total
    vec_send(3, vec.at[3])
    per_noise = 0.5 / hypers[1]
    nat_out[...] = 0.5 * nat[...] + vec_sum(2, vec.at[1]) * per_noise
    vec[4] = vec_sum(3, vec.at[3])
    vec_send(4, vec.at[4])

    pltpu.make_async_copy(own.at[0], own.at[0], own_sem.at[0]).wait()

    @pl.when(both == 1)
    def _():
        pltpu.make_async_copy(own.at[1], own.at[1], own_sem.at[1]).wait()
        own[0] = own[0] + own[1]

    gap = ((z * 2 + lo) * 4 + y) * 64 - mine * 1024
    for i in range(8):
        rows = slice(8 * i, 8 * i + 8)
        shape = (8, 1024)
        same = lax.broadcasted_iota(jnp.int32, shape, 1) - lax.broadcasted_iota(jnp.int32, shape, 0) == gap + 8 * i
        out[rows] = 0.5 * prec[rows] + (jnp.where(same, 0.5, 0.0) + own[0, rows].astype(F32) * per_noise)

    points = 64.0 * count
    total = jnp.sum(vec_sum(4, vec.at[4]), axis=(0, 1), keepdims=True) + hypers[0] * points
    noise = jnp.full((1, 1), hypers[1], F32)
    fit_out[...] = -0.5 * jnp.log(2.0 * jnp.pi * noise) - total / (2.0 * noise * points)
    for k in range(5):
        into = vec_into(k)
        remote(into, into, v_s.at[k], v_r.at[k], partner).wait_send()
    cov_sends(0, cov_sent)

    @pl.when(both == 1)
    def _():
        cov_sends(1, cov_sent)

    for k, (src, dst, sem, to) in enumerate(sends):

        @pl.when(flat(to) != me)
        def _(k=k, src=src, dst=dst, sem=sem, to=to):
            remote(src, dst, f_s.at[k], sem, to).wait_send()

    for c in pm_copies:
        c.wait_send()
    for c in (over, near, on, to_partner):
        c.wait_send()

    def drain(t, carry):
        for c in y1_copies(t) + y2_copies(t) + q1_copies(t) + q2_copies(t):
            c.wait_send()
        for c in (z_all(t), x_copy(t), qz_all(t), qx_copy(t)):
            c.wait_send()
        return carry

    lax.fori_loop(0, ROUNDS, drain, 0)
    lax.fori_loop(0, 4, lambda g, c: (gather_all(g).wait_send(), c)[1], 0)


def step(hypers, ind_t, pts, tgt, scale, mean, whitening, cov, prec, nat):
    dma = pltpu.SemaphoreType.DMA
    n = pts.shape[1]
    return pl.pallas_call(
        kernel,
        out_shape=tuple(jax.ShapeDtypeStruct(s, F32) for s in ((64, 1024), (8, 128), (1, 1))),
        in_specs=[pl.BlockSpec(memory_space=pltpu.SMEM)] + [VMEM] * 5 + [ANY] + [VMEM] * 3,
        out_specs=(VMEM, VMEM, VMEM),
        scratch_shapes=[
            pltpu.VMEM((4, 64, 1024), F32),
            pltpu.VMEM((64, n), BF16),
            pltpu.VMEM(tgt.shape, F32),
            pltpu.VMEM((2, 1024, 2048), BF16),
            pltpu.VMEM((2, 2048, n), BF16),
            pltpu.VMEM((1024, n), F32),
            pltpu.VMEM((8, 128), F32),
            pltpu.VMEM((1, n), F32),
            pltpu.VMEM((9, 64, 128), F32),
            pltpu.VMEM((3, 1024, n), BF16),
            pltpu.VMEM((ROUNDS, 256, 1024), BF16),
            pltpu.VMEM((ROUNDS, 2, 32, 1024), BF16),
            pltpu.VMEM((ROUNDS, 2, 64, 1024), BF16),
            pltpu.VMEM((ROUNDS, 64, 1024), BF16),
            pltpu.VMEM((ROUNDS, 7, 64, 128), BF16),
            pltpu.VMEM((ROUNDS, 64, 128), F32),
            pltpu.VMEM((ROUNDS, 32, 128), BF16),
            pltpu.VMEM((ROUNDS, 32, 128), BF16),
            pltpu.VMEM((ROUNDS, 256, 1024), BF16),
            pltpu.VMEM((ROUNDS, 128, 1024), BF16),
            pltpu.VMEM((ROUNDS, 128, 1024), BF16),
            pltpu.VMEM((ROUNDS, 2, 16, 1024), BF16),
            pltpu.VMEM((ROUNDS, 2, 32, 1024), BF16),
            pltpu.VMEM((ROUNDS, 32, 1024), BF16),
            pltpu.VMEM((ROUNDS, 7, 32, 128), BF16),
            pltpu.VMEM((3, 128, 128), BF16),
            pltpu.VMEM((2, 128, 128), BF16),
            pltpu.VMEM((2, 64, 1024), BF16),
            pltpu.VMEM((3, 1, n), F32),
            pltpu.VMEM((5, 8, 128), F32),
            pltpu.VMEM((3, 8, 128), F32),
            pltpu.VMEM((7, 8, 128), F32),
            pltpu.VMEM((1, 8, 128), F32),
            pltpu.VMEM((15, 8, 128), F32),
            pltpu.VMEM((15, 8, 128), F32),
            dma((5,)), dma((5,)), dma((3,)), dma((16,)), dma,
            dma((4,)), dma((4,)), dma, dma,
            dma((ROUNDS, 2)), dma((ROUNDS, 2)), dma((ROUNDS, 2)), dma((ROUNDS, 2)),
            dma((ROUNDS,)), dma((ROUNDS,)), dma((ROUNDS,)), dma((ROUNDS,)),
            dma((ROUNDS,)), dma((ROUNDS,)), dma((ROUNDS, 2)), dma((ROUNDS, 2)),
            dma((ROUNDS, 2)), dma((ROUNDS, 2)), dma((ROUNDS,)), dma((ROUNDS,)),
            dma((3,)), dma((3,)), dma((9,)), dma((2,)), dma((5,)), dma((5,)),
        ],
        compiler_params=pltpu.CompilerParams(has_side_effects=True, collective_id=0, vmem_limit_bytes=56 * 2**20),
        name="gp_step",
    )(hypers, ind_t, pts, tgt, scale, mean, whitening, cov, prec, nat)


def shards(points, targets, inducing, whitening, mean_v, covariance, precision, natural_one, lengthscales, hypers):
    own_rows, own_points = inducing.shape[0], points.shape[0]
    precision_new, natural_new, expected_fit = step(
        hypers,
        inducing.T,
        points.T,
        targets.reshape(own_points // 128, 128),
        lengthscales.reshape(1, -1),
        mean_v.reshape(8, 128),
        whitening,
        covariance.T,
        precision.T,
        natural_one.reshape(8, 128),
    )
    return precision_new.T, natural_new.reshape(own_rows), expected_fit.reshape(())


def solution(mesh):
    finer = Mesh(mesh.devices.reshape(8, 2, mesh.shape["rep"], 2, 2), AXES)
    return jax.shard_map(
        shards,
        mesh=finer,
        in_specs=(
            P(DP_REP, None), P(DP_REP), P(IND, None), P(IND, None), P(IND),
            P(IND, DP_REP), P(IND, DP_REP), P(IND), P(), P(),
        ),
        out_specs=(P(IND, DP_REP), P(IND), P()),
        check_vma=False,
    )
```

time: 132 us -> 115 us (0.87)
  matrix products: 10.7 us -> 0 us
  other arithmetic: 7.34 us -> 0 us
  Pallas kernels: 105 us -> 109 us
  between operations: 5.31 us -> 2.32 us
    dot_general x2 -> x0, matrix products: 10.7 us -> none  [the longest x1 7.7 us: shards(): white = jnp.dot(whitening, cross, preferred_element_type=F32).astype(BF16)]
    convert_element_type x2 -> x0, other arithmetic: 5.9 us -> none  [the longest x1 4.18 us: shards(): (signal * jnp.exp(-0.5 * (norm_z[:, None] + norm_x[None, :] - 2.0 * inner...]
    pallas_call x2 -> x1, Pallas kernels: 105 us -> 109 us  [step(): pl.pallas_call(kernel, out_shape=tuple((jax.ShapeDtypeStruct(s, F32) for...]
    unnamed x23 -> x2, local copies, waits for them, and re-layouts: 1.35 us -> 2.95 us
where the time goes in v3:
time: 115 us
  Pallas kernels  109 us (95%)
  local copies, waits for them, and re-layouts  2.95 us (3%)
  between operations  2.32 us (2%)
    pallas_call x1, Pallas kernels, step(): pl.pallas_call(kernel, out_shape=tuple((jax.ShapeDtypeStruct(s, F32) for...  109 us
    unnamed x2, local copies, waits for them, and re-layouts  2.95 us

profile of v3, /device:TPU:1, one launch (start us, length us, event | category | flops | bytes accessed | tf_op | source)
XLA Modules:
  0.0 114.6 jit_solution(1724488367750147330)
XLA Ops:
  0.6 109.3 %gp_step.1 = (f32[64,1024]{1,0:T(8,128)}, f32[8,128]{1,0:T(8,128)}, f32[1,1]{1,0:T(1,128)}) custom-call(f32[2]{0:T(128)} %hypers.1, f32[64,1024]{1,0:T(8,128)} %bitcast.12, bf16[64,768]{1,0:T(8,128)(2,1)} %bitcast.15, f32[6,128]{1,0:T(8,128)} %bitcast.16, f32[1,64]{1,0:T(1,128)} %bitcast.20, f32[8,128]{1,0:T(8,128)} %bitcast.17, ...), custom_call_target="tpu_custom_call" | custom-call | tf_op jit(solution)/shard_map/gp_step/pallas_call | solution.py:554
  110.0 1.7 %copy.16 = f32[1024,64]{0,1:T(8,128)} copy(f32[1024,64]{0,1:T(8,128)} %bitcast.11) | data formatting | bytes 524288
  111.6 1.3 %copy.17 = f32[1024]{0:T(1024)} copy(f32[1024]{0:T(1024)} %bitcast.19) | data formatting | bytes 8192

commit v4 on v3

--- a/solution.py
+++ b/solution.py
@@ -15,6 +15,8 @@
 F32 = jnp.float32
 BF16 = jnp.bfloat16
 ROUNDS = 5
+TALL = (32, 32, 32, 48, 16)
+PIECES = ((0, 32), (32, 48), (80, 32), (112, 16))
 
 
 def place():
@@ -58,7 +60,7 @@
     wbuf, pay, y1, y2, zs, zr, xk, xs, xr, qay, qx, qs, q1, q2, qz, qr, fin, fint, own, pmr, vec, vy, vz, vx, va, vb,
     i_s, i_r, c_s, cov_s, cov_r,
     g_s, g_r, p_s, p_r, y1_s, y1_r, y2_s, y2_r, z_s, z_r, x_s, x_r,
-    qx_s, qx_r, q1_s, q1_r, q2_s, q2_r, qz_s, qz_r, pm_s, pm_r, f_s, own_sem, v_s, v_r,
+    qx_s, qx_r, q1_s, q1_r, q2_s, q2_r, qz_s, qz_r, dz_s, dz_r, dq_s, pm_s, pm_r, f_s, own_sem, v_s, v_r,
 ):
     z, lo, y, hi, core = place()
     mine = hi * 2 + core
@@ -102,15 +104,26 @@
         + [owner(16 * mine + 2 * z + e, nxt) for e in range(2)]
         + [owner(16 * high + here + core, low)]
         + [owner(16 * low + 2 * z + e, high) for e in range(2)]
+        + [owner(16 * mine + 2 * z + e, mine) for e in range(2)]
     )
+
+    def ahead(half):
+        return (z - 2 * y - half + 8) % 8
+
+    def formed(half):
+        return 1 - jnp.minimum(ahead(half) // 5, 1)
+
+    alone = equal(ahead(lo), 0) + jnp.minimum(ahead(lo) // 4, 1)
+    needed = [formed(lo)] * 2 + [1] * 7 + [1 - alone] * 2
     own_group, own_q = z // 2, (z % 2) * 8 + lo * 4 + y
     is_d, is_n, is_p = equal(own_group, mine), equal(own_group, nxt), equal(own_group, prv)
     is_s = 1 - is_d - is_n - is_p
-    mirrored = is_p + is_s * core
     both = is_s * core
 
     def cov_target(i, second):
         e = own_q % 2
+        far = is_d * jnp.minimum((i - own_q // 2 + 8) % 8 // 5, 1)
+        mirrored = is_p + is_s * core + far
         to_core = is_p * (own_group % 2) + is_s * ((1 - core) * e + core * second) + (1 - is_p - is_s) * core
         to = (
             (1 - mirrored) * i + mirrored * (own_q // 2),
@@ -119,17 +132,19 @@
             is_p * (own_group // 2) + (1 - is_p) * hi,
             to_core,
         )
-        slot = is_d * e + is_n * (2 + e) + is_p * (4 + e) + is_s * ((1 - core) * 6 + core * (7 + e))
-        return to, cov.at[:, pl.ds(pl.multiple_of(i * 128, 128), 128)], covb.at[slot]
-
+        slot = is_d * e + far * 9 + is_n * (2 + e) + is_p * (4 + e) + is_s * ((1 - core) * 6 + core * (7 + e))
+        return to, cov.at[:, pl.ds(pl.multiple_of(i * 128, 128), 128)], covb.at[slot], cov_r.at[is_d + far]
+
+    covb[...] = jnp.zeros(covb.shape, F32)
+    fin[...] = jnp.zeros(fin.shape, BF16)
     barrier = pltpu.get_barrier_semaphore()
     arrivals = 17 + 8 * (1 + both)
     for to in over_y + over_z + line:
         pl.semaphore_signal(barrier, inc=1, device_id=to, device_id_type=MESH)
-    for to in holders:
-        arrivals = arrivals - equal(flat(to), me)
-
-        @pl.when(flat(to) != me)
+    for to, need in zip(holders, needed):
+        arrivals = arrivals - need * equal(flat(to), me)
+
+        @pl.when(need * (1 - equal(flat(to), me)) == 1)
         def _(to=to):
             pl.semaphore_signal(barrier, inc=1, device_id=to, device_id_type=MESH)
 
@@ -146,15 +161,15 @@
 
     def cov_sends(second, act):
         def one(i, carry):
-            to, src, dst = cov_target(i, second)
+            to, src, dst, sem = cov_target(i, second)
 
             @pl.when(flat(to) != me)
             def _():
-                act(remote(src, dst, cov_s.at[8 * second + i], cov_r, to), True)
+                act(remote(src, dst, cov_s.at[8 * second + i], sem, to), True)
 
             @pl.when(flat(to) == me)
             def _():
-                act(pltpu.make_async_copy(src, dst, cov_r), False)
+                act(pltpu.make_async_copy(src, dst, sem), False)
 
             return carry
 
@@ -200,11 +215,6 @@
     near.start()
     own_z = pltpu.make_async_copy(ind_t, zall.at[mine], c_s.at[2])
     own_z.start()
-    cov_sends(0, cov_start)
-
-    @pl.when(both == 1)
-    def _():
-        cov_sends(1, cov_start)
 
     @pl.when(hi == 1)
     def _():
@@ -253,18 +263,31 @@
             acc[rows, cols] = dot(wv[0, rows, :], cross[0, :, cols], (1, 0))
         return carry
 
+    lax.fori_loop(0, 3, first_half, 0)
     over.wait_recv()
     on.start()
-    lax.fori_loop(0, 4, first_half, 0)
+    cov_sends(0, cov_start)
+
+    @pl.when(both == 1)
+    def _():
+        cov_sends(1, cov_start)
+
+    lax.fori_loop(3, 4, first_half, 0)
     cross_rows(other, 1, core)
     on.wait_recv()
     cross_rows((1 - hi) * 2 + 1 - core, 1, 1 - core)
     w_copies[1].wait()
     square[...] = jnp.zeros((8, 128), F32)
 
-    def gather_piece(g, k):
-        rows = pl.ds(pl.multiple_of(k * 128 + 32 * g, 32), 32)
-        return remote(wbuf.at[core, rows], wbuf.at[2, rows], g_s.at[g], g_r.at[g], gather_to)
+    def gather_start(c):
+        first, size = PIECES[c]
+
+        def one(k, carry):
+            rows = pl.ds(pl.multiple_of(k * 128 + first, 16), size)
+            remote(wbuf.at[core, rows], wbuf.at[2, rows], g_s.at[c], g_r.at[c], gather_to).start()
+            return carry
+
+        lax.fori_loop(0, 8, one, 0)
 
     def second_half(g, carry):
         rows = [pl.ds(pl.multiple_of(k * 128 + 32 * g, 32), 32) for k in range(8)]
@@ -278,24 +301,19 @@
             wide = part.astype(F32)
             both = jnp.sum((wide * wide).reshape(32, 8, 256), axis=0)
             square[...] += both[:, :128] + both[:, 128:]
-        lax.fori_loop(0, 8, lambda k, c: (gather_piece(g, k).start(), c)[1], 0)
+        for c, done in enumerate((0, 2, 3, 3)):
+
+            @pl.when(g == done)
+            def _(c=c):
+                gather_start(c)
+
         return carry
 
     lax.fori_loop(0, 4, second_half, 0)
     to_partner = remote(wbuf.at[core], wbuf.at[core], p_s, p_r, partner)
     to_partner.start()
-    m_row = jnp.concatenate([mean[j : j + 1, :] for j in range(8)], axis=1)
-    pmv[...] = jnp.sum(dot(tile_of(m_row), wbuf[core], (1, 0)), axis=0, keepdims=True)
-    pm_to = (partner, (z, 1 - lo, y, 1 - hi, core), (z, 1 - lo, y, 1 - hi, 1 - core))
-    pm_copies = [remote(pmv, pmr.at[k], pm_s.at[k], pm_r.at[k], to) for k, to in enumerate(pm_to)]
-    for c in pm_copies:
-        c.start()
-    proj = jnp.sum(dot(tile_of(t_row), wbuf[core], (1, 1)), axis=0, keepdims=True)
-    vec[2] = jnp.concatenate([proj[:, 128 * j : 128 * j + 128] for j in range(8)], axis=0)
-    vec_send(0, vec.at[2])
-
     def gather_all(g):
-        rows = pl.ds(0, 256)
+        rows = pl.ds(0, 8 * PIECES[g][1])
         return remote(wbuf.at[core, rows], wbuf.at[2, rows], g_s.at[g], g_r.at[g], gather_to)
 
     up_y, down_y = (z, lo, yp, hi, core), (z, lo, ym, hi, core)
@@ -304,45 +322,82 @@
     def block(k, size):
         return pl.ds(pl.multiple_of(k * size, size), size)
 
+    def wide(t):
+        return pl.ds(0, 640 if t < 2 else 1024)
+
     def y1_copies(t):
-        return (
-            remote(pay.at[t, block(2 * y2p, 32)], y1.at[t, 0], y1_s.at[t, 0], y1_r.at[t, 0], up_y),
-            remote(pay.at[t, block(2 * y2p + 1, 32)], y1.at[t, 1], y1_s.at[t, 1], y1_r.at[t, 1], down_y),
+        h, w = TALL[t], wide(t)
+        return tuple(
+            remote(pay.at[t, block(2 * y2p + k, h), w], y1.at[t, k, pl.ds(0, h), w], y1_s.at[t, k], y1_r.at[t, k], to)
+            for k, to in enumerate((up_y, down_y))
         )
 
     def y2_copies(t):
-        return (
-            remote(pay.at[t, block(yp, 64)], y2.at[t, 0], y2_s.at[t, 0], y2_r.at[t, 0], up_y),
-            remote(pay.at[t, block(ym, 64)], y2.at[t, 1], y2_s.at[t, 1], y2_r.at[t, 1], down_y),
+        h, w = 2 * TALL[t], wide(t)
+        return tuple(
+            remote(pay.at[t, block(at, h), w], y2.at[t, k, pl.ds(0, h), w], y2_s.at[t, k], y2_r.at[t, k], to)
+            for k, (at, to) in enumerate(((yp, up_y), (ym, down_y)))
         )
 
+    def d_copies(t, second):
+        halves = (lo,) if second else (0, 1)
+        out = []
+        for h, half in enumerate(halves):
+            for d in range(5):
+                to = (2 * y + half + d) % 8
+                slot = (to - z + 7) % 8
+                cols = slice(128 * d, 128 * d + 128)
+                if second:
+                    c = (qz.at[t, :, cols], qr.at[t, slot], dq_s.at[t, d], qz_r.at[t])
+                else:
+                    rows = pl.ds(32 * h, 32)
+                    c = (zs.at[t, rows, cols], zr.at[t, slot, rows], dz_s.at[t, 5 * h + d], dz_r.at[t, h])
+                out.append((to, c))
+        return out
+
+    def d_act(t, second, act):
+        for to, c in d_copies(t, second):
+
+            @pl.when(to != z)
+            def _(to=to, c=c):
+                act(remote(*c, (to, lo, y, hi, core)))
+
     def z_send(t):
+        if t < 2:
+            d_act(t, 0, lambda c: c.start())
+            return
         for d in range(1, 8):
             to = (z + d) % 8
-            remote(zs.at[t, :, block(to, 128)], zr.at[t, d - 1], z_s.at[t], z_r.at[t], over_z[d - 1]).start()
+            rows = pl.ds(0, 2 * TALL[t])
+            remote(zs.at[t, rows, block(to, 128)], zr.at[t, d - 1, rows], z_s.at[t], z_r.at[t], over_z[d - 1]).start()
 
     def z_all(t):
-        return remote(zr.at[t], zr.at[t], z_s.at[t], z_r.at[t], over_x)
+        part = zr.at[t, :, pl.ds(0, 2 * TALL[t])]
+        return remote(part, part, z_s.at[t], z_r.at[t], over_x)
 
     def x_copy(t):
-        return remote(xs.at[t], xr.at[t], x_s.at[t], x_r.at[t], over_x)
+        rows = pl.ds(0, TALL[t])
+        return remote(xs.at[t, rows], xr.at[t, rows], x_s.at[t], x_r.at[t], over_x)
 
     def qx_copy(t):
-        return remote(qay.at[t, block(1 - lo, 128)], qx.at[t], qx_s.at[t], qx_r.at[t], over_x)
+        return remote(qay.at[t, block(1 - lo, 128), wide(t)], qx.at[t, :, wide(t)], qx_s.at[t], qx_r.at[t], over_x)
 
     def q1_copies(t):
         return (
-            remote(qs.at[t, block(2 * y2p, 16)], q1.at[t, 0], q1_s.at[t, 0], q1_r.at[t, 0], up_y),
-            remote(qs.at[t, block(2 * y2p + 1, 16)], q1.at[t, 1], q1_s.at[t, 1], q1_r.at[t, 1], down_y),
+            remote(qs.at[t, block(2 * y2p, 16), wide(t)], q1.at[t, 0, :, wide(t)], q1_s.at[t, 0], q1_r.at[t, 0], up_y),
+            remote(qs.at[t, block(2 * y2p + 1, 16), wide(t)], q1.at[t, 1, :, wide(t)], q1_s.at[t, 1], q1_r.at[t, 1], down_y),
         )
 
     def q2_copies(t):
         return (
-            remote(qs.at[t, block(yp, 32)], q2.at[t, 0], q2_s.at[t, 0], q2_r.at[t, 0], up_y),
-            remote(qs.at[t, block(ym, 32)], q2.at[t, 1], q2_s.at[t, 1], q2_r.at[t, 1], down_y),
+            remote(qs.at[t, block(yp, 32), wide(t)], q2.at[t, 0, :, wide(t)], q2_s.at[t, 0], q2_r.at[t, 0], up_y),
+            remote(qs.at[t, block(ym, 32), wide(t)], q2.at[t, 1, :, wide(t)], q2_s.at[t, 1], q2_r.at[t, 1], down_y),
         )
 
     def qz_send(t):
+        if t < 2:
+            d_act(t, 1, lambda c: c.start())
+            return
         for d in range(1, 8):
             to = (z + d) % 8
             remote(qz.at[t, :, block(to, 128)], qr.at[t, d - 1], qz_s.at[t], qz_r.at[t], over_z[d - 1]).start()
@@ -350,118 +405,157 @@
     def qz_all(t):
         return remote(qr.at[t], qr.at[t], qz_s.at[t], qz_r.at[t], over_x)
 
-    def slab(t, g, groups, into):
+    def slab(t, first, h, groups, into):
         is_b, is_h, _ = round_of(t)
         plain = 1 - is_h
         left = is_b * 2 + is_h + plain * (1 - is_b) * core
         right = plain * core
-        shift = g + is_h * 2 * core
-        a = jnp.concatenate([wbuf[left, pl.ds(pl.multiple_of(k * 128 + 32 * shift, 32), 32), :] for k in groups], axis=0)
+        first = first + is_h * 64 * core
+        a = jnp.concatenate([wbuf[left, pl.ds(pl.multiple_of(k * 128 + first, 16), h), :] for k in groups], axis=0)
         for j in range(4):
             b = wbuf[right, j * 256 : (j + 1) * 256, :]
-            part = dot(a, b, (1, 1))
-            into[t, :, j * 256 : (j + 1) * 256] = part.astype(BF16)
-
-    def compute(t):
+            part = dot(a, b, (1, 1)).astype(BF16)
+            if t > 1:
+                into[t, : 8 * h, j * 256 : (j + 1) * 256] = part
+                continue
+            for r, k in enumerate(groups):
+                for h in range(2):
+                    d = (2 * j + h - k) % 8
+                    if d < 5:
+                        into[t, 32 * r : 32 * r + 32, 128 * d : 128 * d + 128] = part[
+                            32 * r : 32 * r + 32, 128 * h : 128 * h + 128
+                        ]
+
+    def qx_start(t):
         is_b, is_h, g = round_of(t)
 
-        @pl.when(is_h == 1)
-        def _():
+        if t == 2:
             to_partner.wait_recv()
-
-        @pl.when(is_b == 1)
-        def _():
+        if t > 2:
+            gather_all(g).wait_recv()
+        slab(t, PIECES[g][0] if t > 2 else 32 * g, 32, (0, 2, 4, 6, 1, 3, 5, 7), qay)
+        qx_copy(t).start()
+
+    def y1_start(t):
+        is_b, is_h, g = round_of(t)
+
+        if t > 2:
             gather_all(g + 1).wait_recv()
-
-        slab(t, g + 1, (0, 2, 4, 6, 1, 3, 5, 7), qay)
-        qx_copy(t).start()
-
-        @pl.when(is_b == 1)
-        def _():
-            gather_all(g).wait_recv()
-
-        slab(t, g, range(8), pay)
+        slab(t, PIECES[g + 1][0] if t > 2 else 32 * (g + 1), TALL[t], range(8), pay)
         for c in y1_copies(t):
             c.start()
 
-    def after_1(t):
+    def after_qx(t):
         qx_copy(t).wait_recv()
-        qs[t] = (qay[t, block(lo, 128), :].astype(F32) + qx[t].astype(F32)).astype(BF16)
+        w = wide(t)
+        qs[t, :, w] = (qay[t, block(lo, 128), w].astype(F32) + qx[t, :, w].astype(F32)).astype(BF16)
         for c in q1_copies(t):
             c.start()
+
+    def after_y1(t):
         for k, c in enumerate(y1_copies(t)):
             c.wait_recv()
-            rows = block(2 * (yp, ym)[k] + k, 32)
-            pay[t, rows, :] = (pay[t, rows, :].astype(F32) + y1[t, k].astype(F32)).astype(BF16)
+            h, w = TALL[t], wide(t)
+            rows = block(2 * (yp, ym)[k] + k, h)
+            pay[t, rows, w] = (pay[t, rows, w].astype(F32) + y1[t, k, :h, w].astype(F32)).astype(BF16)
         for c in y2_copies(t):
             c.start()
 
-    def after_2(t):
+    def after_q1(t):
         for k, c in enumerate(q1_copies(t)):
             c.wait_recv()
             rows = block(2 * (yp, ym)[k] + k, 16)
-            qs[t, rows, :] = (qs[t, rows, :].astype(F32) + q1[t, k].astype(F32)).astype(BF16)
+            w = wide(t)
+            qs[t, rows, w] = (qs[t, rows, w].astype(F32) + q1[t, k, :, w].astype(F32)).astype(BF16)
         for c in q2_copies(t):
             c.start()
+
+    def after_y2(t):
         for c in y2_copies(t):
             c.wait_recv()
-        total = pay[t, block(y, 64), :].astype(F32) + y2[t, 0].astype(F32) + y2[t, 1].astype(F32)
-        zs[t] = total.astype(BF16)
+        h, w = 2 * TALL[t], wide(t)
+        total = pay[t, block(y, h), w].astype(F32) + y2[t, 0, :h, w].astype(F32) + y2[t, 1, :h, w].astype(F32)
+        zs[t, :h, w] = total.astype(BF16)
         z_send(t)
 
-    def after_3(t):
+    def after_q2(t):
         for c in q2_copies(t):
             c.wait_recv()
-        total = qs[t, block(y, 32), :].astype(F32) + q2[t, 0].astype(F32) + q2[t, 1].astype(F32)
-        qz[t] = total.astype(BF16)
+        w = wide(t)
+        total = qs[t, block(y, 32), w].astype(F32) + q2[t, 0, :, w].astype(F32) + q2[t, 1, :, w].astype(F32)
+        qz[t, :, w] = total.astype(BF16)
         qz_send(t)
+
+    def after_z(t):
+        if t < 2:
+            for h in range(2):
+                rows = pl.ds(32 * h, 32)
+
+                @pl.when(formed(h) == 1)
+                def _(h=h, rows=rows):
+                    remote(zr.at[t, :, rows], zr.at[t, :, rows], x_s.at[t], dz_r.at[t, h], over_x).wait_recv()
+                    total = zs[t, rows, block(jnp.minimum(ahead(h), 4), 128)].astype(F32)
+                    xk[t, rows, :] = total + sum(zr[t, d, rows].astype(F32) for d in range(7))
+
+            @pl.when(formed(1 - lo) == 1)
+            def _():
+                xs[t, :32] = xk[t, block(1 - lo, 32), :].astype(BF16)
+                x_copy(t).start()
+
+            return
         z_all(t).wait_recv()
-        total = zs[t, :, block(z, 128)].astype(F32)
+        h = TALL[t]
+        total = zs[t, : 2 * h, block(z, 128)].astype(F32)
         for d in range(7):
-            total = total + zr[t, d].astype(F32)
-        xk[t] = total
-        xs[t] = xk[t, block(1 - lo, 32), :].astype(BF16)
+            total = total + zr[t, d, : 2 * h].astype(F32)
+        xk[t, : 2 * h] = total
+        xs[t, :h] = xk[t, block(1 - lo, h), :].astype(BF16)
         x_copy(t).start()
 
-    def after_4(t):
+    def finish(t, second, total):
         is_b, is_h, g = round_of(t)
-        slot = is_b + 2 * is_h
-        row = g + is_h * core * 2
-        x_copy(t).wait_recv()
-        total = xk[t, block(lo, 32), :] + xr[t].astype(F32)
-        fin[slot, block(row, 32), :] = total.astype(BF16)
+        first = PIECES[g + second][0] if t > 2 else 32 * (g + second)
+        rows = pl.ds(pl.multiple_of(first + is_h * core * 64, 16), total.shape[0])
+        fin[is_b + 2 * is_h, rows, :] = total.astype(BF16)
+
+    def after_qz(t):
+        if t < 2:
+
+            @pl.when(formed(lo) == 1)
+            def _():
+                qz_all(t).wait_recv()
+                total = qz[t, :, block(jnp.minimum(ahead(lo), 4), 128)].astype(F32)
+                finish(t, 0, total + sum(qr[t, d].astype(F32) for d in range(7)))
+
+            return
         qz_all(t).wait_recv()
         total = qz[t, :, block(z, 128)].astype(F32)
         for d in range(7):
             total = total + qr[t, d].astype(F32)
-        fin[slot, block(row + 1, 32), :] = total.astype(BF16)
-
-    zero = jnp.zeros((128, 128), BF16)
-    fin[2] = zero
-
-    def step(t, carry):
-        @pl.when(t == 3)
-        def _():
-            vec[0] = vec_sum(0, vec.at[2])
-            vec_send(1, vec.at[0])
-
-        @pl.when(t == 6)
-        def _():
-            vec[1] = vec_sum(1, vec.at[0])
-            vec_send(2, vec.at[1])
-
-        for lag, work in ((8, after_4), (6, after_3), (4, after_2), (2, after_1), (0, compute)):
-
-            @pl.when((t >= lag) & (t < ROUNDS + lag))
-            def _(lag=lag, work=work):
-                work(t - lag)
-
-        return carry
-
-    lax.fori_loop(0, ROUNDS + 8, step, 0)
-
-    fint[0] = fin[1].astype(F32).T.astype(BF16)
-    fint[1] = fin[2].astype(F32).T.astype(BF16)
+        finish(t, 0, total)
+
+    def after_x(t):
+        def add():
+            x_copy(t).wait_recv()
+            h = TALL[t]
+            finish(t, 1, xk[t, block(lo, h), :] + xr[t, :h].astype(F32))
+
+        if t < 2:
+            pl.when(formed(lo) == 1)(add)
+        else:
+            add()
+
+    pm_to = (partner, (z, 1 - lo, y, 1 - hi, core), (z, 1 - lo, y, 1 - hi, 1 - core))
+    pm_copies = [remote(pmv, pmr.at[k], pm_s.at[k], pm_r.at[k], to) for k, to in enumerate(pm_to)]
+
+    def means_and_proj():
+        m_row = jnp.concatenate([mean[j : j + 1, :] for j in range(8)], axis=1)
+        pmv[...] = jnp.sum(dot(tile_of(m_row), wbuf[core], (1, 0)), axis=0, keepdims=True)
+        for c in pm_copies:
+            c.start()
+        proj = jnp.sum(dot(tile_of(t_row), wbuf[core], (1, 1)), axis=0, keepdims=True)
+        vec[2] = jnp.concatenate([proj[:, 128 * j : 128 * j + 128] for j in range(8)], axis=0)
+        vec_send(0, vec.at[2])
 
     direct = block(z, 128)
     mirror = block(2 * y + lo, 128)
@@ -469,29 +563,71 @@
     pieces = [fin.at[0, pl.ds(64 * e, 64)] for e in range(2)] + [fin.at[1, pl.ds(64 * e, 64)] for e in range(2)]
     pieces += [fint.at[0, pl.ds(64 * e, 64)] for e in range(2)]
     pieces += [fin.at[2, half]] + [fint.at[1, pl.ds(64 * e, 64)] for e in range(2)]
+    pieces += [fint.at[2, pl.ds(64 * e, 64)] for e in range(2)]
     places = [own.at[0, :, direct]] * 4 + [own.at[0, :, mirror]] * 2 + [own.at[0, :, direct]] + [own.at[core, :, mirror]] * 2
-    sems = [own_sem.at[0]] * 7 + [own_sem.at[core]] * 2
+    places += [own.at[0, :, mirror]] * 2
+    sems = [own_sem.at[0]] * 7 + [own_sem.at[core]] * 2 + [own_sem.at[0]] * 2
     sends = list(zip(pieces, places, sems, holders))
 
-    for k, (src, dst, sem, to) in enumerate(sends):
-
-        @pl.when(flat(to) != me)
-        def _(k=k, src=src, dst=dst, sem=sem, to=to):
-            remote(src, dst, f_s.at[k], sem, to).start()
-
-        @pl.when(flat(to) == me)
-        def _(src=src, dst=dst, sem=sem):
-            pltpu.make_async_copy(src, dst, sem).start()
-
-    for c in pm_copies:
-        c.wait_recv()
-    resid = t_row - (pmv[...] + pmr[0] + pmr[1] + pmr[2])
-    resid = resid * resid
-    total = sum(resid[:, 128 * j : 128 * j + 128] for j in range(count // 128))
-    total = jnp.broadcast_to(total / 32, (8, 128)) - square[...]
-    pltpu.make_async_copy(covb, covb, cov_r).wait()
-    for k, piece in enumerate(pieces):
-        total = total + jnp.sum((covb[k] * piece[...].astype(F32)).reshape(8, 8, 128), axis=0)
+    def deliver(some):
+        for k in some:
+            src, dst, sem, to = sends[k]
+
+            @pl.when(needed[k] * (1 - equal(flat(to), me)) == 1)
+            def _(k=k, src=src, dst=dst, sem=sem, to=to):
+                remote(src, dst, f_s.at[k], sem, to).start()
+
+            @pl.when(needed[k] * equal(flat(to), me) == 1)
+            def _(src=src, dst=dst, sem=sem):
+                pltpu.make_async_copy(src, dst, sem).start()
+
+        return sum(
+            jnp.sum((covb[k] * pieces[k][...].astype(F32)).reshape(8, 8, 128), axis=0) for k in some
+        )
+
+    def early():
+        for c in pm_copies:
+            c.wait_recv()
+        resid = t_row - (pmv[...] + pmr[0] + pmr[1] + pmr[2])
+        resid = resid * resid
+        total = sum(resid[:, 128 * j : 128 * j + 128] for j in range(count // 128))
+        total = jnp.broadcast_to(total / 32, (8, 128)) - square[...]
+        fint[1] = fin[2].astype(F32).T.astype(BF16)
+        fint[2] = fin[0].astype(F32).T.astype(BF16)
+        for k, first, last in ((0, 2, 9), (1, 0, 2), (2, 9, 11)):
+            some = covb.at[pl.ds(first, last - first)]
+
+            @pl.when(needed[first] == 1)
+            def _(k=k, some=some):
+                pltpu.make_async_copy(some, some, cov_r.at[k]).wait()
+
+        return total + deliver((0, 1, 6, 7, 8, 9, 10))
+
+    order = (
+        (qx_start, 0), (y1_start, 0), (qx_start, 1), (y1_start, 1), (qx_start, 2), (y1_start, 2), (qx_start, 3),
+        (after_qx, 0), (after_y1, 0), (after_y1, 1), (after_y1, 2), (after_q1, 0), (after_qx, 1), (after_y2, 0),
+        (after_y2, 1), (after_qx, 2), (after_y2, 2), (after_q2, 0), (after_q1, 1), (y1_start, 3), (after_z, 0),
+        (after_q1, 2), (after_z, 1), (after_q2, 1), (after_qx, 3), (after_x, 0), (after_x, 1), (after_y1, 3),
+        (after_z, 2), (after_q2, 2), (after_qz, 0), (after_q1, 3), (after_qz, 1), (qx_start, 4), (after_x, 2),
+        (after_y2, 3), (after_qz, 2), (y1_start, 4), (after_q2, 3), (after_y1, 4), (after_qx, 4), (after_y2, 4),
+        (after_q1, 4), (after_z, 3), (after_qz, 3), (after_x, 3), (after_q2, 4), (after_z, 4), (after_x, 4),
+        (after_qz, 4),
+    )
+    for at, (work, t) in enumerate(order):
+        if at == 4:
+            means_and_proj()
+        if at == 12:
+            vec[0] = vec_sum(0, vec.at[2])
+            vec_send(1, vec.at[0])
+        if at == 24:
+            vec[1] = vec_sum(1, vec.at[0])
+            vec_send(2, vec.at[1])
+        work(t)
+        if at == 36:
+            partial = early()
+
+    fint[0] = fin[1].astype(F32).T.astype(BF16)
+    total = partial + deliver((2, 3, 4, 5))
     vec[3] = total
     vec_send(3, vec.at[3])
     per_noise = 0.5 / hypers[1]
@@ -528,7 +664,7 @@
 
     for k, (src, dst, sem, to) in enumerate(sends):
 
-        @pl.when(flat(to) != me)
+        @pl.when(needed[k] * (1 - equal(flat(to), me)) == 1)
         def _(k=k, src=src, dst=dst, sem=sem, to=to):
             remote(src, dst, f_s.at[k], sem, to).wait_send()
 
@@ -537,15 +673,18 @@
     for c in (over, near, on, to_partner):
         c.wait_send()
 
-    def drain(t, carry):
-        for c in y1_copies(t) + y2_copies(t) + q1_copies(t) + q2_copies(t):
+    for t in range(ROUNDS):
+        for c in y1_copies(t) + y2_copies(t) + q1_copies(t) + q2_copies(t) + (qx_copy(t),):
             c.wait_send()
-        for c in (z_all(t), x_copy(t), qz_all(t), qx_copy(t)):
-            c.wait_send()
-        return carry
-
-    lax.fori_loop(0, ROUNDS, drain, 0)
-    lax.fori_loop(0, 4, lambda g, c: (gather_all(g).wait_send(), c)[1], 0)
+        if t < 2:
+            d_act(t, 0, lambda c: c.wait_send())
+            d_act(t, 1, lambda c: c.wait_send())
+            pl.when(formed(1 - lo) == 1)(x_copy(t).wait_send)
+        else:
+            for c in (z_all(t), x_copy(t), qz_all(t)):
+                c.wait_send()
+    for c in range(4):
+        gather_all(c).wait_send()
 
 
 def step(hypers, ind_t, pts, tgt, scale, mean, whitening, cov, prec, nat):
@@ -565,16 +704,16 @@
             pltpu.VMEM((1024, n), F32),
             pltpu.VMEM((8, 128), F32),
             pltpu.VMEM((1, n), F32),
-            pltpu.VMEM((9, 64, 128), F32),
+            pltpu.VMEM((11, 64, 128), F32),
             pltpu.VMEM((3, 1024, n), BF16),
-            pltpu.VMEM((ROUNDS, 256, 1024), BF16),
-            pltpu.VMEM((ROUNDS, 2, 32, 1024), BF16),
-            pltpu.VMEM((ROUNDS, 2, 64, 1024), BF16),
-            pltpu.VMEM((ROUNDS, 64, 1024), BF16),
-            pltpu.VMEM((ROUNDS, 7, 64, 128), BF16),
-            pltpu.VMEM((ROUNDS, 64, 128), F32),
-            pltpu.VMEM((ROUNDS, 32, 128), BF16),
-            pltpu.VMEM((ROUNDS, 32, 128), BF16),
+            pltpu.VMEM((ROUNDS, 8 * max(TALL), 1024), BF16),
+            pltpu.VMEM((ROUNDS, 2, max(TALL), 1024), BF16),
+            pltpu.VMEM((ROUNDS, 2, 2 * max(TALL), 1024), BF16),
+            pltpu.VMEM((ROUNDS, 2 * max(TALL), 1024), BF16),
+            pltpu.VMEM((ROUNDS, 7, 2 * max(TALL), 128), BF16),
+            pltpu.VMEM((ROUNDS, 2 * max(TALL), 128), F32),
+            pltpu.VMEM((ROUNDS, max(TALL), 128), BF16),
+            pltpu.VMEM((ROUNDS, max(TALL), 128), BF16),
             pltpu.VMEM((ROUNDS, 256, 1024), BF16),
             pltpu.VMEM((ROUNDS, 128, 1024), BF16),
             pltpu.VMEM((ROUNDS, 128, 1024), BF16),
@@ -583,7 +722,7 @@
             pltpu.VMEM((ROUNDS, 32, 1024), BF16),
             pltpu.VMEM((ROUNDS, 7, 32, 128), BF16),
             pltpu.VMEM((3, 128, 128), BF16),
-            pltpu.VMEM((2, 128, 128), BF16),
+            pltpu.VMEM((3, 128, 128), BF16),
             pltpu.VMEM((2, 64, 1024), BF16),
             pltpu.VMEM((3, 1, n), F32),
             pltpu.VMEM((5, 8, 128), F32),
@@ -592,13 +731,14 @@
             pltpu.VMEM((1, 8, 128), F32),
             pltpu.VMEM((15, 8, 128), F32),
             pltpu.VMEM((15, 8, 128), F32),
-            dma((5,)), dma((5,)), dma((3,)), dma((16,)), dma,
+            dma((5,)), dma((5,)), dma((3,)), dma((16,)), dma((3,)),
             dma((4,)), dma((4,)), dma, dma,
             dma((ROUNDS, 2)), dma((ROUNDS, 2)), dma((ROUNDS, 2)), dma((ROUNDS, 2)),
             dma((ROUNDS,)), dma((ROUNDS,)), dma((ROUNDS,)), dma((ROUNDS,)),
             dma((ROUNDS,)), dma((ROUNDS,)), dma((ROUNDS, 2)), dma((ROUNDS, 2)),
             dma((ROUNDS, 2)), dma((ROUNDS, 2)), dma((ROUNDS,)), dma((ROUNDS,)),
-            dma((3,)), dma((3,)), dma((9,)), dma((2,)), dma((5,)), dma((5,)),
+            dma((2, 10)), dma((2, 2)), dma((2, 5)),
+            dma((3,)), dma((3,)), dma((11,)), dma((2,)), dma((5,)), dma((5,)),
         ],
         compiler_params=pltpu.CompilerParams(has_side_effects=True, collective_id=0, vmem_limit_bytes=56 * 2**20),
         name="gp_step",

time: 115 us -> 102 us (0.89)
  Pallas kernels: 109 us -> 96.8 us
    pallas_call x1, Pallas kernels: 109 us -> 96.8 us  [step(): pl.pallas_call(kernel, out_shape=tuple((jax.ShapeDtypeStruct(s, F32) for...]
where the time goes in v4:
time: 102 us
  Pallas kernels  96.8 us (95%)
  local copies, waits for them, and re-layouts  2.95 us (3%)
  between operations  2.32 us (2%)
    pallas_call x1, Pallas kernels, step(): pl.pallas_call(kernel, out_shape=tuple((jax.ShapeDtypeStruct(s, F32) for...  96.8 us
    unnamed x2, local copies, waits for them, and re-layouts  2.95 us

profile of v4, /device:TPU:1, one launch (start us, length us, event | category | flops | bytes accessed | tf_op | source)
XLA Modules:
  0.0 102.1 jit_solution(13000478631593946407)
XLA Ops:
  0.6 96.8 %gp_step.1 = (f32[64,1024]{1,0:T(8,128)}, f32[8,128]{1,0:T(8,128)}, f32[1,1]{1,0:T(1,128)}) custom-call(f32[2]{0:T(128)} %hypers.1, f32[64,1024]{1,0:T(8,128)} %bitcast.12, bf16[64,768]{1,0:T(8,128)(2,1)} %bitcast.15, f32[6,128]{1,0:T(8,128)} %bitcast.16, f32[1,64]{1,0:T(1,128)} %bitcast.20, f32[8,128]{1,0:T(8,128)} %bitcast.17, ...), custom_call_target="tpu_custom_call" | custom-call | tf_op jit(solution)/shard_map/gp_step/pallas_call | solution.py:693
  97.5 1.7 %copy.16 = f32[1024,64]{0,1:T(8,128)} copy(f32[1024,64]{0,1:T(8,128)} %bitcast.11) | data formatting | bytes 524288
  99.1 1.3 %copy.17 = f32[1024]{0:T(1024)} copy(f32[1024]{0:T(1024)} %bitcast.19) | data formatting | bytes 8192

commit v5 on v4

--- a/solution.py
+++ b/solution.py
@@ -57,7 +57,7 @@
 def kernel(
     hypers, ind_t, pts_in, tgt_in, scale_in, mean, whitening, cov, prec, nat, out, nat_out, fit_out,
     zall, pts, tgt, wv, cross, acc, square, pmv, covb,
-    wbuf, pay, y1, y2, zs, zr, xk, xs, xr, qay, qx, qs, q1, q2, qz, qr, fin, fint, own, pmr, vec, vy, vz, vx, va, vb,
+    wbuf, pay, y1, y2, zs, zr, xk, xs, xr, qay, qx, qs, q1, q2, qz, qr, fin, fint, own, pmr, vec, vy, vz, vx, va, vb, row,
     i_s, i_r, c_s, cov_s, cov_r,
     g_s, g_r, p_s, p_r, y1_s, y1_r, y2_s, y2_r, z_s, z_r, x_s, x_r,
     qx_s, qx_r, q1_s, q1_r, q2_s, q2_r, qz_s, qz_r, dz_s, dz_r, dq_s, pm_s, pm_r, f_s, own_sem, v_s, v_r,
@@ -628,12 +628,12 @@
 
     fint[0] = fin[1].astype(F32).T.astype(BF16)
     total = partial + deliver((2, 3, 4, 5))
-    vec[3] = total
-    vec_send(3, vec.at[3])
+    row[0] = jnp.sum(total, axis=0, keepdims=True)
+    vec_send(3, row.at[0])
     per_noise = 0.5 / hypers[1]
     nat_out[...] = 0.5 * nat[...] + vec_sum(2, vec.at[1]) * per_noise
-    vec[4] = vec_sum(3, vec.at[3])
-    vec_send(4, vec.at[4])
+    row[1] = vec_sum(3, row.at[0])
+    vec_send(4, row.at[1])
 
     pltpu.make_async_copy(own.at[0], own.at[0], own_sem.at[0]).wait()
 
@@ -650,7 +650,7 @@
         out[rows] = 0.5 * prec[rows] + (jnp.where(same, 0.5, 0.0) + own[0, rows].astype(F32) * per_noise)
 
     points = 64.0 * count
-    total = jnp.sum(vec_sum(4, vec.at[4]), axis=(0, 1), keepdims=True) + hypers[0] * points
+    total = jnp.sum(vec_sum(4, row.at[1]), axis=(0, 1), keepdims=True) + hypers[0] * points
     noise = jnp.full((1, 1), hypers[1], F32)
     fit_out[...] = -0.5 * jnp.log(2.0 * jnp.pi * noise) - total / (2.0 * noise * points)
     for k in range(5):
@@ -725,12 +725,13 @@
             pltpu.VMEM((3, 128, 128), BF16),
             pltpu.VMEM((2, 64, 1024), BF16),
             pltpu.VMEM((3, 1, n), F32),
-            pltpu.VMEM((5, 8, 128), F32),
+            pltpu.VMEM((3, 8, 128), F32),
             pltpu.VMEM((3, 8, 128), F32),
             pltpu.VMEM((7, 8, 128), F32),
             pltpu.VMEM((1, 8, 128), F32),
-            pltpu.VMEM((15, 8, 128), F32),
-            pltpu.VMEM((15, 8, 128), F32),
+            pltpu.VMEM((15, 1, 128), F32),
+            pltpu.VMEM((15, 1, 128), F32),
+            pltpu.VMEM((2, 1, 128), F32),
             dma((5,)), dma((5,)), dma((3,)), dma((16,)), dma((3,)),
             dma((4,)), dma((4,)), dma, dma,
             dma((ROUNDS, 2)), dma((ROUNDS, 2)), dma((ROUNDS, 2)), dma((ROUNDS, 2)),

time: 102 us -> 101 us (level)
  Pallas kernels: 96.8 us -> 95.3 us
    pallas_call x1, Pallas kernels: 96.8 us -> 95.3 us  [step(): pl.pallas_call(kernel, out_shape=tuple((jax.ShapeDtypeStruct(s, F32) for...]
where the time goes in v5:
time: 101 us
  Pallas kernels  95.3 us (94%)
  local copies, waits for them, and re-layouts  2.95 us (3%)
  between operations  2.32 us (2%)
    pallas_call x1, Pallas kernels, step(): pl.pallas_call(kernel, out_shape=tuple((jax.ShapeDtypeStruct(s, F32) for...  95.3 us
    unnamed x2, local copies, waits for them, and re-layouts  2.95 us

profile of v5, /device:TPU:1, one launch (start us, length us, event | category | flops | bytes accessed | tf_op | source)
XLA Modules:
  0.0 100.6 jit_solution(16686551627482964606)
XLA Ops:
  0.6 95.3 %gp_step.1 = (f32[64,1024]{1,0:T(8,128)}, f32[8,128]{1,0:T(8,128)}, f32[1,1]{1,0:T(1,128)}) custom-call(f32[2]{0:T(128)} %hypers.1, f32[64,1024]{1,0:T(8,128)} %bitcast.12, bf16[64,768]{1,0:T(8,128)(2,1)} %bitcast.15, f32[6,128]{1,0:T(8,128)} %bitcast.16, f32[1,64]{1,0:T(1,128)} %bitcast.20, f32[8,128]{1,0:T(8,128)} %bitcast.17, ...), custom_call_target="tpu_custom_call" | custom-call | tf_op jit(solution)/shard_map/gp_step/pallas_call | solution.py:693
  96.0 1.7 %copy.16 = f32[1024,64]{0,1:T(8,128)} copy(f32[1024,64]{0,1:T(8,128)} %bitcast.11) | data formatting | bytes 524288
  97.6 1.3 %copy.17 = f32[1024]{0:T(1024)} copy(f32[1024]{0:T(1024)} %bitcast.19) | data formatting | bytes 8192
